TPU v7x, 32 devices: a whole 2x2x4 slice. The times are simulated.
32 devices in a mesh: grp: 2 (over y), tok: 4 (over z), feat: 4 (over x, core).
Axes of the slice: x: 2, y: 2, z: 4, core: 2. Of those that a mesh axis runs over, the one named last changes fastest.
Arguments:
- acts: bfloat16 [6144, 28672], P(('grp', 'tok'), 'feat'), parts along dimension 0, may hold values from -6 to 6
- grads: bfloat16 [6144, 8192], P(('grp', 'tok'), 'feat'), parts along dimension 0, may hold values from -6 to 6
- proj_in: bfloat16 [28672, 512], P('feat'), may hold values from -0.03125 to 0.03125
- proj_out: bfloat16 [8192, 512], P('feat'), may hold values from -0.0625 to 0.0625
- doc_lengths: int32 [8], P('grp'), parts along dimension 0, may hold values from 1 to 1536, 3072 in all
- doc_owner: int32 [8], P('grp'), parts along dimension 0, may hold values from 0 to 3, as said below
Outputs:
- doc_grads: float32 [8, 512, 512], P(('grp', 'tok'), 'feat'), parts along dimension 0
There are 2 independent parts, one for each index of `grp`. A program takes and returns all parts, laid end to end along the dimension named above; an argument that names none is the same for every part. Nothing has to cross between parts.
Inputs may be any that keep to these rules, and one draw needn't show every extreme that they name: `doc_lengths`: the lengths sum to 3072; the largest is exactly 1536. `doc_owner`: every index along tok owns exactly 1 documents.
All inputs are finite; a program needn't handle non-finite values.
Results may differ from a plain program's by a relative error of at most 0.0043.
Values may be sent and summed in bfloat16 or wider, within the bound.
No kernel may reach another device: no remote copies, remote signals or barrier semaphores. Data moves between devices by JAX's collectives and lax.ppermute only.
A program may use at most 64 MiB of HBM per device.

v0:
```python
import jax
import jax.numpy as jnp
from jax import lax
from jax.sharding import PartitionSpec as P


def outer_sum(weight_cols, low_out, low_in):
    width = weight_cols.shape[1]
    row_share = low_out.shape[1]
    weighted = (low_out[:, None, :] * weight_cols[:, :, None]).reshape(
        low_out.shape[0], width * row_share
    )
    product = lax.dot_general(
        weighted, low_in, (((0,), (0,)), ((), ())), preferred_element_type=jnp.float32
    )
    return product.reshape(width, row_share, low_in.shape[1])


def shards(acts, grads, proj_in, proj_out, doc_lengths, doc_owner):
    tok_rows = acts.shape[0]
    doc_count = doc_lengths.shape[0]
    slot_count = doc_count // lax.axis_size("tok")
    part_in = jnp.dot(acts, proj_in, preferred_element_type=jnp.float32)
    part_out = jnp.dot(grads, proj_out, preferred_element_type=jnp.float32)
    full_in = lax.psum(part_in, "feat")
    grad_part = lax.psum_scatter(part_out, "feat", scatter_dimension=1, tiled=True)
    in_low = full_in.astype(jnp.bfloat16)
    out_low = grad_part.astype(jnp.bfloat16)
    doc_ends = jnp.cumsum(doc_lengths)
    doc_starts = doc_ends - doc_lengths
    doc_index = jnp.arange(doc_count, dtype=jnp.int32)
    same_owner = doc_owner[:, None] == doc_owner[None, :]
    earlier = doc_index[:, None] < doc_index[None, :]
    slot_rank = jnp.sum((same_owner & earlier).astype(jnp.int32), axis=0)
    target = doc_owner * slot_count + slot_rank
    matches = target[:, None] == doc_index[None, :]
    routing = matches.astype(jnp.bfloat16)
    own_first = lax.axis_index("tok") * slot_count
    position = lax.axis_index("tok") * tok_rows + jnp.arange(tok_rows, dtype=jnp.int32)
    member = (
        (position[:, None] >= doc_starts[None, :]) & (position[:, None] < doc_ends[None, :])
    ).astype(jnp.bfloat16)
    all_weights = jnp.dot(member, routing, preferred_element_type=jnp.float32).astype(jnp.bfloat16)
    totals = lax.psum_scatter(
        outer_sum(all_weights, out_low, in_low), "tok", scatter_dimension=0, tiled=True
    )
    slot_lengths = jnp.sum(jnp.where(matches, doc_lengths[:, None], 0), axis=0)
    own_lengths = lax.dynamic_slice_in_dim(slot_lengths, own_first, slot_count, 0)
    scaling = lax.rsqrt(own_lengths.astype(jnp.float32))
    return totals * scaling[:, None, None]


def solution(mesh):
    in_specs = (
        P(("grp", "tok"), "feat"),
        P(("grp", "tok"), "feat"),
        P("feat", None),
        P("feat", None),
        P("grp"),
        P("grp"),
    )
    out_specs = P(("grp", "tok"), "feat", None)
    return jax.shard_map(shards, mesh=mesh, in_specs=in_specs, out_specs=out_specs, check_vma=False)
```

profile of v0, /device:TPU:0, one launch (start us, length us, event | category | flops | bytes accessed | tf_op | source)
XLA Modules:
  0.0 109.7 jit_solution(2129140301364226923)
XLA Ops:
  6.5 0.0 copy-start
  6.5 0.0 copy-start.1
  6.5 0.0 reduce-scatter.3.cloned.1.call-start
  6.5 1.9 %copy-done = bf16[768,2048]{1,0:T(8,128)(2,1)S(1)} copy-done((bf16[768,2048]{1,0:T(8,128)(2,1)S(1)}, bf16[768,2048]{1,0:T(8,128)(2,1)}, u32[]{:S(2)}) %copy-start) | copy-done | bytes 3145752
  8.4 4.5 %fusion.15 = f32[768,512]{1,0:T(8,128)} fusion(bf16[768,2048]{1,0:T(8,128)(2,1)S(1)} %copy-done, bf16[2048,512]{1,0:T(8,128)(2,1)} %param.9), kind=kOutput, calls=%fused_computation.23 | convolution fusion | flops 1610612736 | bytes 6815744 | tf_op jit(solution)/shard_map/dot_general | solution.py:24
  13.0 0.0 reduce-scatter.3.cloned.1.call-update
  13.0 0.0 reduce-scatter.5.cloned.1.call-start
  13.0 0.0 copy-done.1
  13.1 0.1 convert_reduce_fusion
  13.1 0.0 copy-start.2
  13.1 11.6 %fusion.16 = f32[768,512]{1,0:T(8,128)} fusion(bf16[768,7168]{1,0:T(8,128)(2,1)} %param.6, bf16[7168,512]{1,0:T(8,128)(2,1)} %param.8), kind=kOutput, calls=%fused_computation.24 | convolution fusion | flops 5637144576 | bytes 19922944 | tf_op jit(solution)/shard_map/dot_general | solution.py:23
  24.8 0.0 copy-done.2
  24.8 0.2 reduce-window.8
  25.0 0.3 convolution_convert_fusion
  25.2 43.7 %all-reduce.1 = bf16[768,512]{1,0:T(8,128)(2,1)} all-reduce(f32[768,512]{1,0:T(8,128)} %fusion.16), channel_id=1, replica_groups=mesh['grp'=2,'tok'=4,'feat'=4] {'feat'}, use_global_device_ids=true, to_apply=%region_3.4 | all-reduce | flops 393216 | bytes 2359296 | tf_op jit(solution)/shard_map/psum | solution.py:25
  68.9 0.0 reduce-scatter.3.cloned.1.call-done
  68.9 1.0 convert_element_type.17
  70.0 0.1 copy.9
  70.1 2.7 %fusion = f32[4,128,512]{2,1,0:T(8,128)} fusion(bf16[768,512]{1,0:T(8,128)(2,1)} %all-reduce.1, bf16[768,4]{0,1:T(4,128)(2,1)S(1)} %convolution_convert_fusion, bf16[768,128]{0,1:T(8,128)(2,1)S(1)} %copy.9), kind=kOutput, calls=%fused_computation.1 | convolution fusion | flops 403046400 | bytes 2037760 | tf_op jit(solution)/shard_map/dot_general | solution.py:13
  72.8 0.0 reduce-scatter.5.cloned.1.call-update
  72.8 0.1 select_reduce_fusion
  72.9 0.6 dynamic_slice.3
  74.2 26.9 %reduce-scatter.5.cloned.1.call-done = f32[1,128,512]{2,1,0:T(8,128)} async-done(((f32[4,128,512]{2,1,0:T(8,128)}), f32[1,128,512]{2,1,0:T(8,128)}) %reduce-scatter.5.cloned.1.call-update) | async-done | bytes 262160 | tf_op jit(solution)/shard_map/reduce_scatter | solution.py:44
  101.1 1.7 %broadcast_multiply_fusion = f32[1,128,512]{2,1,0:T(8,128)} fusion(f32[1,128,512]{2,1,0:T(8,128)} %reduce-scatter.5.cloned.1.call-done, f32[]{:T(128)} %bitcast.6), kind=kLoop, calls=%fused_computation.8 | loop fusion | flops 65536 | bytes 524292 | tf_op jit(solution)/shard_map/mul | solution.py:50
  (3 shorter events, 0.0 us)
Async XLA Ops:
  6.5 1.9 %copy-start = (bf16[768,2048]{1,0:T(8,128)(2,1)S(1)}, bf16[768,2048]{1,0:T(8,128)(2,1)}, u32[]{:S(2)}) copy-start(bf16[768,2048]{1,0:T(8,128)(2,1)} %param.7) | copy-start | bytes 9437188
  6.5 6.5 %copy-start.1 = (s32[4]{0:T(128)S(1)}, s32[4]{0:T(128)}, u32[]{:S(2)}) copy-start(s32[4]{0:T(128)} %param.11) | copy-start | bytes 52
  6.5 62.4 %reduce-scatter.3.cloned.1.call-start = ((), (), s32[]{:S(2)}) async-start(), calls=%async_computation.2 | async-start | bytes 1966080 | tf_op jit(solution)/shard_map/reduce_scatter | solution.py:26
  13.0 88.2 %reduce-scatter.5.cloned.1.call-start = ((), (), s32[]{:S(2)}) async-start(), calls=%async_computation.3 | async-start | bytes 1310720 | tf_op jit(solution)/shard_map/reduce_scatter | solution.py:44
  13.1 11.6 %copy-start.2 = (s32[4]{0:T(128)S(1)}, s32[4]{0:T(128)}, u32[]{:S(2)}) copy-start(s32[4]{0:T(128)} %param.10) | copy-start | bytes 52
Sparse Core Ops, SparseCore 0:
  13.1 39.2 reduce-scatter.2
  73.0 28.1 reduce-scatter.4
where the time goes:
time: 110 us
  blocking collectives  43.7 us (40%)
  waiting for transfers between devices  27 us (25%)
  matrix products  19.1 us (17%)
  between operations  14.1 us (13%)
  other arithmetic  3.05 us (3%)
  local copies, waits for them, and re-layouts  2.62 us (2%)
    psum x1, blocking collectives, shards(): full_in = lax.psum(part_in, 'feat')  43.7 us
    reduce_scatter x1, waiting for transfers between devices, shards(): lax.psum_scatter(outer_sum(all_weights, out_low, in_low), 'tok', scatter_...  26.9 us
    dot_general x1, matrix products, shards(): part_in = jnp.dot(acts, proj_in, preferred_element_type=jnp.float32)  11.6 us
    dot_general x1, matrix products, shards(): part_out = jnp.dot(grads, proj_out, preferred_element_type=jnp.float32)  4.54 us
    dot_general x1, matrix products, outer_sum(): lax.dot_general(weighted, low_in, (((0,), (0,)), ((), ())), preferred_ele...  2.7 us
  transfers between devices with their start and end apart: 2, of which 1 were waited for; matrix products, arithmetic and copies ran while one was open for 12% of the time, Pallas kernels for 0%

commit v1 on v0

v1 whole, which is shorter than its diff:
```python
import functools

import jax
import jax.numpy as jnp
from jax import lax
from jax.experimental import pallas as pl
from jax.experimental.pallas import tpu as pltpu
from jax.sharding import PartitionSpec as P


CHUNKS = 2
FIRST = 2
MIB = 1 << 20


def partner_pairs(size):
    return [(i, i ^ 1) for i in range(size)]


def chip_shift(size, step):
    chips = size // 2
    return [(i, ((i // 2 + step) % chips) * 2 + i % 2) for i in range(size)]


def exchange(size, step):
    if size & (size - 1) == 0:
        return [(i, i ^ step) for i in range(size)]
    return [(i, (i + step) % size) for i in range(size)]


def receiver(size, me, step):
    return me ^ step if size & (size - 1) == 0 else (me + step) % size


def depth_tile(depth, most):
    tile = most // 128 * 128
    while depth % tile:
        tile -= 128
    return tile


def split_by_core(core, product, share, groups, mine_ref, theirs_ref):
    for which in range(2):

        @pl.when(core == which)
        def _():
            for group in range(groups):
                place = pl.ds(group * share, share)
                mine_ref[:, place] = product[:, pl.ds((2 * group + which) * share, share)]
                theirs_ref[:, place] = product[:, pl.ds((2 * group + 1 - which) * share, share)]


def grads_kernel(chips, core_ref, a_hbm, w_hbm, mine_ref, theirs_ref, a_ref, w_ref, total, sems):
    depth, rank = w_ref.shape
    tile = depth_tile(depth, 512)
    copies = []
    for t in range(depth // tile):
        lines = pl.ds(t * tile, tile)
        group = (
            pltpu.make_async_copy(a_hbm.at[:, lines], a_ref.at[:, lines], sems.at[0, t]),
            pltpu.make_async_copy(w_hbm.at[lines, :], w_ref.at[lines, :], sems.at[1, t]),
        )
        for copy in group:
            copy.start()
        copies.append(group)
    for t in range(depth // tile):
        lines = pl.ds(t * tile, tile)
        for copy in copies[t]:
            copy.wait()
        product = jnp.dot(a_ref[:, lines], w_ref[lines, :], preferred_element_type=jnp.float32)
        if t == 0:
            total[...] = product
        else:
            total[...] += product
    split_by_core(core_ref[0], total, rank // (2 * chips), chips, mine_ref, theirs_ref)


def project_grads(grads, proj_out, core, chips):
    rows, depth = grads.shape
    rank = proj_out.shape[1]
    count = depth // depth_tile(depth, 512)
    half = pltpu.VMEM((rows, rank // 2), jnp.float32)
    return pl.pallas_call(
        functools.partial(grads_kernel, chips),
        in_specs=[pl.BlockSpec(memory_space=pltpu.SMEM)]
        + [pl.BlockSpec(memory_space=pltpu.HBM)] * 2,
        out_specs=[pl.BlockSpec(memory_space=pltpu.VMEM)] * 2,
        out_shape=[half, half],
        scratch_shapes=[
            pltpu.VMEM((rows, depth), grads.dtype),
            pltpu.VMEM((depth, rank), proj_out.dtype),
            pltpu.VMEM((rows, rank), jnp.float32),
            pltpu.SemaphoreType.DMA((2, count)),
        ],
        compiler_params=pltpu.CompilerParams(vmem_limit_bytes=12 * MIB),
        cost_estimate=pl.CostEstimate(
            flops=2 * rows * depth * rank,
            bytes_accessed=2 * (rows * depth + depth * rank),
            transcendentals=0,
        ),
        name="project_grads",
    )(core, grads, proj_out)


def acts_kernel(first, last, begin, core_ref, a_hbm, w_hbm, *refs):
    refs = list(refs)
    refs.pop(0)
    start_ref = None if first else refs.pop(0)
    a_ref, w_ref, total, sems = refs[-4:]
    out_refs = refs[:-4]
    span = w_ref.shape[0]
    tile = depth_tile(span, 1024)
    copies = []
    for t in range(span // tile):
        lines = pl.ds(t * tile, tile)
        far_lines = pl.ds(begin + t * tile, tile)
        group = (
            pltpu.make_async_copy(a_hbm.at[:, far_lines], a_ref.at[:, lines], sems.at[0, t]),
            pltpu.make_async_copy(w_hbm.at[far_lines, :], w_ref.at[lines, :], sems.at[1, t]),
        )
        for copy in group:
            copy.start()
        copies.append(group)
    into = total if last else out_refs[0]
    for t in range(span // tile):
        lines = pl.ds(t * tile, tile)
        for copy in copies[t]:
            copy.wait()
        product = jnp.dot(a_ref[:, lines], w_ref[lines, :], preferred_element_type=jnp.float32)
        if t > 0:
            into[...] += product
        elif first:
            into[...] = product
        else:
            into[...] = start_ref[...] + product
    if last:
        chunks = len(out_refs) // 2
        half, width = out_refs[0].shape
        for chunk in range(chunks):
            columns = pl.ds(chunk * width, width)
            own = pl.ds(pl.multiple_of(core_ref[0] * half, half), half)
            other = pl.ds(pl.multiple_of((1 - core_ref[0]) * half, half), half)
            out_refs[2 * chunk][...] = total[own, columns]
            out_refs[2 * chunk + 1][...] = total[other, columns]


def project_acts(acts, proj_in, core, begin, span, after, start, chunks):
    rows, rank = acts.shape[0], proj_in.shape[1]
    first, last = start is None, begin + span == proj_in.shape[0]
    if last:
        out = [pltpu.VMEM((rows // 2, rank // chunks), jnp.float32)] * (2 * chunks)
    else:
        out = [pltpu.VMEM((rows, rank), jnp.float32)]
    starts = [] if first else [start]
    return pl.pallas_call(
        functools.partial(acts_kernel, first, last, begin),
        in_specs=[pl.BlockSpec(memory_space=pltpu.SMEM)]
        + [pl.BlockSpec(memory_space=pltpu.HBM)] * 2
        + [pl.BlockSpec(memory_space=pl.ANY)]
        + [pl.BlockSpec(memory_space=pltpu.VMEM)] * len(starts),
        out_specs=[pl.BlockSpec(memory_space=pltpu.VMEM)] * len(out),
        out_shape=out,
        scratch_shapes=[
            pltpu.VMEM((rows, span), acts.dtype),
            pltpu.VMEM((span, rank), proj_in.dtype),
            pltpu.VMEM((rows, rank), jnp.float32),
            pltpu.SemaphoreType.DMA((2, span // depth_tile(span, 1024))),
        ],
        compiler_params=pltpu.CompilerParams(vmem_limit_bytes=24 * MIB),
        cost_estimate=pl.CostEstimate(
            flops=2 * rows * span * rank,
            bytes_accessed=2 * span * (rank + rows),
            transcendentals=0,
        ),
        name="project_acts",
    )(core, acts, proj_in, after, *starts)


def spread_kernel(tok_count, core_ref, tok_ref, lengths_ref, owner_ref, low_ref, out_ref):
    rows, share = low_ref.shape
    docs = lengths_ref.shape[0]
    slots = docs // tok_count
    half = rows // 2
    tok, core = tok_ref[0], core_ref[0]
    starts, ends, targets = [], [], []
    seen = jnp.int32(0)
    for d in range(docs):
        starts.append(seen)
        seen = seen + lengths_ref[d]
        ends.append(seen)
        rank = jnp.int32(0)
        for e in range(d):
            rank = rank + (owner_ref[e] == owner_ref[d]).astype(jnp.int32)
        targets.append(owner_ref[d] * slots + rank)
    turned = low_ref[...].astype(jnp.float32).T
    for part in range(2):
        first = (core if part == 0 else 1 - core) * half
        position = tok * rows + first + lax.broadcasted_iota(jnp.int32, (share, half), 1)
        piece = jnp.where(
            core == part, turned[:, :half], turned[:, half:]
        )
        for step in range(tok_count):
            for slot in range(slots):
                want = receiver(tok_count, tok, step) * slots + slot
                begin = end = jnp.int32(0)
                for d in range(docs):
                    hit = targets[d] == want
                    begin = jnp.where(hit, starts[d], begin)
                    end = jnp.where(hit, ends[d], end)
                member = (position >= begin) & (position < end)
                out_ref[pl.ds((step * slots + slot) * share, share), pl.ds(part * half, half)] = (
                    jnp.where(member, piece, 0.0).astype(out_ref.dtype)
                )


def spread(low, core, tok, doc_lengths, doc_owner, tok_count):
    rows, share = low.shape
    docs = doc_lengths.shape[0]
    return pl.pallas_call(
        functools.partial(spread_kernel, tok_count),
        in_specs=[pl.BlockSpec(memory_space=pltpu.SMEM)] * 4
        + [pl.BlockSpec(memory_space=pltpu.VMEM)],
        out_specs=pl.BlockSpec(memory_space=pltpu.VMEM),
        out_shape=pltpu.VMEM((docs * share, rows), jnp.bfloat16),
        compiler_params=pltpu.CompilerParams(vmem_limit_bytes=6 * MIB),
        cost_estimate=pl.CostEstimate(flops=10**6, bytes_accessed=0, transcendentals=0),
        name="spread",
    )(core, tok, doc_lengths, doc_owner, low)


def product_kernel(w_ref, own_ref, other_ref, kept_ref, *sent_refs):
    half = own_ref.shape[0]
    size = kept_ref.shape[0]
    product = jnp.dot(w_ref[:, :half], own_ref[...], preferred_element_type=jnp.float32)
    product += jnp.dot(w_ref[:, half:], other_ref[...], preferred_element_type=jnp.float32)
    kept_ref[...] = product[:size]
    for i, ref in enumerate(sent_refs):
        ref[...] = product[(i + 1) * size : (i + 2) * size].astype(ref.dtype)


def outer_products(spread_low, own, other, tok_count):
    size = spread_low.shape[0] // tok_count
    width = own.shape[1]
    return pl.pallas_call(
        product_kernel,
        in_specs=[pl.BlockSpec(memory_space=pltpu.VMEM)] * 3,
        out_specs=[pl.BlockSpec(memory_space=pltpu.VMEM)] * tok_count,
        out_shape=[pltpu.VMEM((size, width), jnp.float32)]
        + [pltpu.VMEM((size, width), jnp.bfloat16)] * (tok_count - 1),
        compiler_params=pltpu.CompilerParams(vmem_limit_bytes=6 * MIB),
        cost_estimate=pl.CostEstimate(
            flops=2 * spread_low.shape[0] * spread_low.shape[1] * width,
            bytes_accessed=0,
            transcendentals=0,
        ),
        name="outer_products",
    )(spread_low, own, other)


def finish_kernel(tok_count, tok_ref, lengths_ref, owner_ref, *refs):
    total_refs, out_ref = refs[:-1], refs[-1]
    docs = lengths_ref.shape[0]
    slots = docs // tok_count
    share = out_ref.shape[1]
    tok = tok_ref[0]
    for slot in range(slots):
        length = jnp.int32(0)
        for d in range(docs):
            rank = jnp.int32(0)
            for e in range(d):
                rank = rank + (owner_ref[e] == owner_ref[d]).astype(jnp.int32)
            hit = (owner_ref[d] == tok) & (rank == slot)
            length = jnp.where(hit, lengths_ref[d], length)
        place = 0
        for chunk in range(CHUNKS):
            parts = total_refs[chunk * tok_count : (chunk + 1) * tok_count]
            width = parts[0].shape[1]
            lines = pl.ds(slot * share, share)
            total = parts[0][lines, :]
            for part in parts[1:]:
                total = total + part[lines, :].astype(jnp.float32)
            scaling = lax.rsqrt(jnp.full((share, width), length, jnp.int32).astype(jnp.float32))
            out_ref[slot, :, pl.ds(place, width)] = total * scaling
            place += width


def finish(parts, tok, doc_lengths, doc_owner, tok_count, share):
    slots = doc_lengths.shape[0] // tok_count
    rank = sum(p.shape[1] for p in parts[::tok_count])
    return pl.pallas_call(
        functools.partial(finish_kernel, tok_count),
        in_specs=[pl.BlockSpec(memory_space=pltpu.SMEM)] * 3
        + [pl.BlockSpec(memory_space=pltpu.VMEM)] * len(parts),
        out_specs=pl.BlockSpec(memory_space=pltpu.VMEM),
        out_shape=jax.ShapeDtypeStruct((slots, share, rank), jnp.float32),
        compiler_params=pltpu.CompilerParams(vmem_limit_bytes=6 * MIB),
        name="finish",
    )(tok, doc_lengths, doc_owner, *parts)


def shards(acts, grads, proj_in, proj_out, doc_lengths, doc_owner):
    depth, rank = proj_in.shape
    tok_count = lax.axis_size("tok")
    feat_count = lax.axis_size("feat")
    chips = feat_count // 2
    feat = lax.axis_index("feat")
    chip = feat // 2
    core = (feat % 2).reshape(1)
    tok = lax.axis_index("tok").reshape(1)
    share = rank // feat_count
    first = depth // 7 * FIRST
    acts, grads, proj_in, proj_out = (
        pltpu.with_memory_space_constraint(v, pltpu.HBM) for v in (acts, grads, proj_in, proj_out)
    )

    def swap(value):
        return lax.ppermute(value, "feat", partner_pairs(feat_count))

    mine, theirs = project_grads(grads, proj_out, core, chips)
    other = swap(theirs)
    pair_out = mine + other
    out_low = lax.dynamic_slice_in_dim(pair_out, chip * share, share, 1)
    sent = [
        lax.dynamic_slice_in_dim(
            pair_out, (chip + step) % chips * share, share, 1
        ).astype(jnp.bfloat16)
        for step in range(1, chips)
    ]
    next_after = sent[0]
    for step in range(1, chips):
        other = lax.ppermute(sent[step - 1], "feat", chip_shift(feat_count, step))
        out_low = out_low + other.astype(jnp.float32)
    out_low = out_low.astype(jnp.bfloat16)

    (held,) = project_acts(acts, proj_in, core, 0, first, theirs, None, CHUNKS)
    halves = project_acts(
        acts, proj_in, core, first, depth - first, next_after, held, CHUNKS
    )
    lows = []
    for chunk in range(CHUNKS):
        mine, theirs = halves[2 * chunk : 2 * chunk + 2]
        other = swap(theirs)
        pair_in = mine + other
        sent = pair_in.astype(jnp.bfloat16)
        full_in = pair_in
        for step in range(1, chips):
            other = lax.ppermute(sent, "feat", chip_shift(feat_count, step))
            full_in = full_in + other.astype(jnp.float32)
        lows.append(full_in.astype(jnp.bfloat16))

    spread_low = spread(out_low, core, tok, doc_lengths, doc_owner, tok_count)
    parts = []
    for low_in in lows:
        other = swap(low_in)
        kept, *sends = outer_products(spread_low, low_in, other, tok_count)
        parts.append(kept)
        for step in range(1, tok_count):
            parts.append(lax.ppermute(sends[step - 1], "tok", exchange(tok_count, step)))
    return finish(parts, tok, doc_lengths, doc_owner, tok_count, share)


def solution(mesh):
    in_specs = (
        P(("grp", "tok"), "feat"),
        P(("grp", "tok"), "feat"),
        P("feat", None),
        P("feat", None),
        P("grp"),
        P("grp"),
    )
    out_specs = P(("grp", "tok"), "feat", None)

    return jax.shard_map(shards, mesh=mesh, in_specs=in_specs, out_specs=out_specs, check_vma=False)
```

time: 110 us -> 50.1 us (0.46)
  blocking collectives: 43.7 us -> 0 us
  matrix products: 19.1 us -> 0 us
  Pallas kernels: 0 us -> 16.4 us
  starting transfers between devices: 0.04 us -> 14.9 us
  between operations: 14.1 us -> 0.15 us
  waiting for transfers between devices: 27 us -> 18 us
  other arithmetic: 3.05 us -> 0.42 us
  local copies, waits for them, and re-layouts: 2.62 us -> 0.05 us
    psum x1 -> x0, blocking collectives: 43.7 us -> none  [shards(): full_in = lax.psum(part_in, 'feat')]
    reduce_scatter x2 -> x0, waiting for transfers between devices: 26.9 us -> none  [the longest x1 26.9 us: shards(): lax.psum_scatter(outer_sum(all_weights, out_low, in_low), 'tok', scatter_...]
    dot_general x4 -> x0, matrix products: 19.1 us -> none  [the longest x1 11.6 us: shards(): part_in = jnp.dot(acts, proj_in, preferred_element_type=jnp.float32)]
    ppermute x0 -> x14, waiting for transfers between devices: none -> 18 us  [the longest x2 11.5 us: shards(): other = lax.ppermute(sent, 'feat', chip_shift(feat_count, step))]
    pallas_call x0 -> x7, Pallas kernels: none -> 16.4 us  [the longest x2 10 us: project_acts(): pl.pallas_call(functools.partial(acts_kernel, first, last, begin), in_spe...]
    ppermute x0 -> x14, starting transfers between devices: none -> 14.9 us  [the longest x6 8.94 us: shards(): lax.ppermute(sends[step - 1], 'tok', exchange(tok_count, step))]
    unnamed x6 -> x4, local copies, waits for them, and re-layouts: 1.89 us -> 0.01 us
    mul x1 -> x0, other arithmetic: 1.67 us -> none  [shards(): return totals * scaling[:, None, None]]
  transfers between devices with their start and end apart: 2 -> 14, of which waited for: 1 -> 4; matrix products, arithmetic and copies ran while one was open for 12% -> 1% of each run, Pallas kernels for 0% -> 10%
where the time goes in v1:
time: 50.1 us; the launch traced here: 49.9 us
  waiting for transfers between devices  18 us (36%)
  Pallas kernels  16.4 us (33%)
  starting transfers between devices  14.9 us (30%)
    ppermute x2, waiting for transfers between devices, shards(): other = lax.ppermute(sent, 'feat', chip_shift(feat_count, step))  11.5 us
    pallas_call x2, Pallas kernels, project_acts(): pl.pallas_call(functools.partial(acts_kernel, first, last, begin), in_spe...  10 us
    ppermute x6, starting transfers between devices, shards(): lax.ppermute(sends[step - 1], 'tok', exchange(tok_count, step))  8.94 us
    ppermute x6, waiting for transfers between devices, shards(): lax.ppermute(sends[step - 1], 'tok', exchange(tok_count, step))  6.53 us
    pallas_call x1, Pallas kernels, project_grads(): pl.pallas_call(functools.partial(grads_kernel, chips), in_specs=[pl.Block...  3.4 us
    ppermute x1, starting transfers between devices, shards(): other = lax.ppermute(sent[step - 1], 'feat', chip_shift(feat_count, step))  2.52 us
    ppermute x2, starting transfers between devices, shards(): other = lax.ppermute(sent, 'feat', chip_shift(feat_count, step))  2.15 us
    pallas_call x1, Pallas kernels, finish(): pl.pallas_call(functools.partial(finish_kernel, tok_count), in_specs=[pl....  1.31 us
  transfers between devices with their start and end apart: 14, of which 4 were waited for; matrix products, arithmetic and copies ran while one was open for 1% of the time, Pallas kernels for 10%

profile of v1, /device:TPU:0, one launch (start us, length us, event | category | flops | bytes accessed | tf_op | source)
XLA Modules:
  0.0 49.9 jit_solution(3333617334964409418)
XLA Ops:
  0.0 3.4 %project_grads.1 = (f32[768,256]{1,0:T(8,128)S(1)}, f32[768,256]{1,0:T(8,128)S(1)}) custom-call(s32[1]{0:T(128)} %bitcast.1.core_ref, bf16[768,2048]{1,0:T(8,128)(2,1)} %a_hbm.3, bf16[2048,512]{1,0:T(8,128)(2,1)} %w_hbm.3), custom_call_target="tpu_custom_call" | custom-call | flops 1610612736 | bytes 5242880 | tf_op jit(solution)/shard_map/project_grads/pallas_call | solution.py:83
  3.4 0.6 %collective-permute-start = (f32[768,256]{1,0:T(8,128)S(1)}, f32[768,256]{1,0:T(8,128)S(1)}, u32[]{:S(2)}, u32[]{:S(2)}) collective-permute-start(f32[768,256]{1,0:T(8,128)S(1)} %get-tuple-element.20.refs_0_), channel_id=1, source_target_pairs={{0,1},{1,0},{2,3},{3,2},{4,5},{5,4},{6,7},{7,6},{8,9},{9,8},{10,11... | collective-permute-start | bytes 2359304 | tf_op jit(solution)/shard_map/ppermute | solution.py:317
  4.0 3.6 %project_acts.2.refs_1_ = f32[768,512]{1,0:T(8,128)S(1)} custom-call(s32[1]{0:T(128)} %bitcast.1.core_ref, bf16[768,7168]{1,0:T(8,128)(2,1)} %a_hbm.5, bf16[7168,512]{1,0:T(8,128)(2,1)} %w_hbm.5, f32[768,256]{1,0:T(8,128)S(1)} %get-tuple-element.20.refs_0_), custom_call_target="tpu_custom_call" | custom-call | flops 1610612736 | bytes 5242880 | tf_op jit(solution)/shard_map/project_acts/pallas_call | solution.py:155
  7.6 0.0 collective-permute-done
  7.6 0.1 add.36
  7.8 6.4 %project_acts.3 = (f32[384,256]{1,0:T(8,128)S(1)}, f32[384,256]{1,0:T(8,128)S(1)}, f32[384,256]{1,0:T(8,128)S(1)}, f32[384,256]{1,0:T(8,128)S(1)}) custom-call(s32[1]{0:T(128)} %bitcast.1.core_ref, bf16[768,7168]{1,0:T(8,128)(2,1)} %a_hbm.5, bf16[7168,512]{1,0:T(8,128)(2,1)} %w_hbm.5, bf16[768,128]{1,0:T(8,128)(2,1)S(1)} %dynamic-slice_convert_fusion.refs_0_, ...), custom_call_target="tpu_custom_call" | custom-call | flops 4026531840 | bytes 13107200 | tf_op jit(solution)/shard_map/project_acts/pallas_call | solution.py:155
  14.2 0.0 copy-start
  14.2 0.0 copy-start.1
  14.2 0.1 collective-permute-start.2
  14.3 0.5 collective-permute-start.8
  14.8 2.5 %collective-permute-start.1 = (bf16[768,128]{1,0:T(8,128)(2,1)S(1)}, bf16[768,128]{1,0:T(8,128)(2,1)S(1)}, u32[]{:S(2)}, u32[]{:S(2)}) collective-permute-start(bf16[768,128]{1,0:T(8,128)(2,1)S(1)} %dynamic-slice_convert_fusion.refs_0_), channel_id=1, source_target_pairs={{0,2},{1,3},{2,0},{3,1},{4,6},{5,7},{6,4},{7,5},{8,10},{9,11},{10,... | collective-permute-start | bytes 589832 | tf_op jit(solution)/shard_map/ppermute | solution.py:331
  17.3 0.0 collective-permute-done.2
  17.3 0.1 fusion.1
  17.4 1.3 %collective-permute-start.3 = (bf16[384,256]{1,0:T(8,128)(2,1)S(1)}, bf16[384,256]{1,0:T(8,128)(2,1)S(1)}, u32[]{:S(2)}, u32[]{:S(2)}) collective-permute-start(bf16[384,256]{1,0:T(8,128)(2,1)S(1)} %get-tuple-element.35), channel_id=1, source_target_pairs={{0,2},{1,3},{2,0},{3,1},{4,6},{5,7},{6,4},{7,5},{8,10},{9,11},{10,... | collective-permute-start | bytes 589832 | tf_op jit(solution)/shard_map/ppermute | solution.py:347
  18.7 0.0 collective-permute-done.8
  18.7 0.1 fusion
  18.8 0.8 %collective-permute-start.9 = (bf16[384,256]{1,0:T(8,128)(2,1)S(1)}, bf16[384,256]{1,0:T(8,128)(2,1)S(1)}, u32[]{:S(2)}, u32[]{:S(2)}) collective-permute-start(bf16[384,256]{1,0:T(8,128)(2,1)S(1)} %get-tuple-element.33), channel_id=1, source_target_pairs={{0,2},{1,3},{2,0},{3,1},{4,6},{5,7},{6,4},{7,5},{8,10},{9,11},{10,... | collective-permute-start | bytes 589832 | tf_op jit(solution)/shard_map/ppermute | solution.py:347
  19.6 7.7 %collective-permute-done.3 = bf16[384,256]{1,0:T(8,128)(2,1)S(1)} collective-permute-done((bf16[384,256]{1,0:T(8,128)(2,1)S(1)}, bf16[384,256]{1,0:T(8,128)(2,1)S(1)}, u32[]{:S(2)}, u32[]{:S(2)}) %collective-permute-start.3) | collective-permute-done | bytes 196640 | tf_op jit(solution)/shard_map/ppermute | solution.py:347
  27.3 0.1 add_convert_fusion.1.own_ref
  27.3 0.1 collective-permute-start.4
  27.4 3.8 %collective-permute-done.9 = bf16[384,256]{1,0:T(8,128)(2,1)S(1)} collective-permute-done((bf16[384,256]{1,0:T(8,128)(2,1)S(1)}, bf16[384,256]{1,0:T(8,128)(2,1)S(1)}, u32[]{:S(2)}, u32[]{:S(2)}) %collective-permute-start.9) | collective-permute-done | bytes 196640 | tf_op jit(solution)/shard_map/ppermute | solution.py:347
  31.2 0.1 add_convert_fusion.own_ref
  31.3 0.1 collective-permute-start.10
  31.4 0.0 collective-permute-done.1
  31.4 0.1 add_convert_fusion.2.low_ref
  31.4 0.0 copy-done
  31.4 0.0 copy-done.1
  31.5 0.8 %spread.1.w_ref = bf16[512,768]{1,0:T(8,128)(2,1)S(1)} custom-call(s32[1]{0:T(128)} %bitcast.1.core_ref, s32[1]{0:T(128)} %bitcast.tok_ref, s32[4]{0:T(128)S(1)} %copy-done, s32[4]{0:T(128)S(1)} %copy-done.1, bf16[768,128]{1,0:T(8,128)(2,1)S(1)} %add_convert_fusion.2.low_ref), custom_call_target="tpu_custom_call" | custom-call | flops 1000000 | tf_op jit(solution)/shard_map/spread/pallas_call | solution.py:219
  32.2 0.0 collective-permute-done.4.other_ref
  32.3 0.4 outer_products.2
  32.7 1.9 %collective-permute-start.5 = (bf16[128,256]{1,0:T(8,128)(2,1)S(1)}, bf16[128,256]{1,0:T(8,128)(2,1)S(1)}, u32[]{:S(2)}, u32[]{:S(2)}) collective-permute-start(bf16[128,256]{1,0:T(8,128)(2,1)S(1)} %get-tuple-element.24), channel_id=1, source_target_pairs={{0,4},{4,0},{8,12},{12,8},{1,5},{5,1},{9,13},{13,9},{2,6},{6,2},{1... | collective-permute-start | bytes 196616 | tf_op jit(solution)/shard_map/ppermute | solution.py:358
  34.6 2.6 %collective-permute-start.6 = (bf16[128,256]{1,0:T(8,128)(2,1)S(1)}, bf16[128,256]{1,0:T(8,128)(2,1)S(1)}, u32[]{:S(2)}, u32[]{:S(2)}) collective-permute-start(bf16[128,256]{1,0:T(8,128)(2,1)S(1)} %get-tuple-element.25), channel_id=1, source_target_pairs={{0,8},{4,12},{8,0},{12,4},{1,9},{5,13},{9,1},{13,5},{2,10},{6,14},... | collective-permute-start | bytes 196616 | tf_op jit(solution)/shard_map/ppermute | solution.py:358
  37.2 0.0 collective-permute-start.7
  37.2 0.0 collective-permute-done.10.other_ref
  37.2 0.4 outer_products.3
  37.6 1.0 %collective-permute-start.11 = (bf16[128,256]{1,0:T(8,128)(2,1)S(1)}, bf16[128,256]{1,0:T(8,128)(2,1)S(1)}, u32[]{:S(2)}, u32[]{:S(2)}) collective-permute-start(bf16[128,256]{1,0:T(8,128)(2,1)S(1)} %get-tuple-element.30), channel_id=1, source_target_pairs={{0,4},{4,0},{8,12},{12,8},{1,5},{5,1},{9,13},{13,9},{2,6},{6,2},{1... | collective-permute-start | bytes 196616 | tf_op jit(solution)/shard_map/ppermute | solution.py:358
  38.6 3.5 %collective-permute-start.12 = (bf16[128,256]{1,0:T(8,128)(2,1)S(1)}, bf16[128,256]{1,0:T(8,128)(2,1)S(1)}, u32[]{:S(2)}, u32[]{:S(2)}) collective-permute-start(bf16[128,256]{1,0:T(8,128)(2,1)S(1)} %get-tuple-element.31), channel_id=1, source_target_pairs={{0,8},{4,12},{8,0},{12,4},{1,9},{5,13},{9,1},{13,5},{2,10},{6,14},... | collective-permute-start | bytes 196616 | tf_op jit(solution)/shard_map/ppermute | solution.py:358
  42.1 0.0 collective-permute-done.5.refs_1_
  42.1 0.0 collective-permute-start.13
  42.1 0.0 collective-permute-done.6.refs_2_
  42.1 1.9 %collective-permute-done.7.refs_3_ = bf16[128,256]{1,0:T(8,128)(2,1)S(1)} collective-permute-done((bf16[128,256]{1,0:T(8,128)(2,1)S(1)}, bf16[128,256]{1,0:T(8,128)(2,1)S(1)}, u32[]{:S(2)}, u32[]{:S(2)}) %collective-permute-start.7) | collective-permute-done | bytes 65568 | tf_op jit(solution)/shard_map/ppermute | solution.py:358
  43.9 0.0 collective-permute-done.11.refs_5_
  43.9 4.7 %collective-permute-done.12.refs_6_ = bf16[128,256]{1,0:T(8,128)(2,1)S(1)} collective-permute-done((bf16[128,256]{1,0:T(8,128)(2,1)S(1)}, bf16[128,256]{1,0:T(8,128)(2,1)S(1)}, u32[]{:S(2)}, u32[]{:S(2)}) %collective-permute-start.12) | collective-permute-done | bytes 65568 | tf_op jit(solution)/shard_map/ppermute | solution.py:358
  48.6 0.0 collective-permute-done.13.refs_7_
  48.6 1.3 %finish.1 = f32[1,128,512]{2,1,0:T(8,128)} custom-call(s32[1]{0:T(128)} %bitcast.tok_ref, s32[4]{0:T(128)S(1)} %copy-done, s32[4]{0:T(128)S(1)} %copy-done.1, f32[128,256]{1,0:T(8,128)S(1)} %get-tuple-element.23.refs_0_, bf16[128,256]{1,0:T(8,128)(2,1)S(1)} %collective-permute-done.5.refs_1_, bf16[128,256]{1,0:T(8,128)(2,1)S(1)} %collective-permute-done.6.refs_2_, ...), custom_call_target="tpu_custom_call" | custom-call | tf_op jit(solution)/shard_map/finish/pallas_call | solution.py:290
  (1 shorter events, 0.0 us)
Async XLA Ops:
  3.4 4.2 %collective-permute-start = (f32[768,256]{1,0:T(8,128)S(1)}, f32[768,256]{1,0:T(8,128)S(1)}, u32[]{:S(2)}, u32[]{:S(2)}) collective-permute-start(f32[768,256]{1,0:T(8,128)S(1)} %get-tuple-element.20.refs_0_), channel_id=1, source_target_pairs={{0,1},{1,0},{2,3},{3,2},{4,5},{5,4},{6,7},{7,6},{8,9},{9,8},{10,11... | collective-permute-start | bytes 2359304 | tf_op jit(solution)/shard_map/ppermute | solution.py:317
  14.2 17.2 %copy-start = (s32[4]{0:T(128)S(1)}, s32[4]{0:T(128)}, u32[]{:S(2)}) copy-start(s32[4]{0:T(128)} %lengths_ref.3) | copy-start | bytes 52
  14.2 17.2 %copy-start.1 = (s32[4]{0:T(128)S(1)}, s32[4]{0:T(128)}, u32[]{:S(2)}) copy-start(s32[4]{0:T(128)} %owner_ref.3) | copy-start | bytes 52
  14.2 3.1 %collective-permute-start.2 = (f32[384,256]{1,0:T(8,128)S(1)}, f32[384,256]{1,0:T(8,128)S(1)}, u32[]{:S(2)}, u32[]{:S(2)}) collective-permute-start(f32[384,256]{1,0:T(8,128)S(1)} %get-tuple-element.22), channel_id=1, source_target_pairs={{0,1},{1,0},{2,3},{3,2},{4,5},{5,4},{6,7},{7,6},{8,9},{9,8},{10,11... | collective-permute-start | bytes 1179656 | tf_op jit(solution)/shard_map/ppermute | solution.py:317
  14.3 4.4 %collective-permute-start.8 = (f32[384,256]{1,0:T(8,128)S(1)}, f32[384,256]{1,0:T(8,128)S(1)}, u32[]{:S(2)}, u32[]{:S(2)}) collective-permute-start(f32[384,256]{1,0:T(8,128)S(1)} %get-tuple-element.28), channel_id=1, source_target_pairs={{0,1},{1,0},{2,3},{3,2},{4,5},{5,4},{6,7},{7,6},{8,9},{9,8},{10,11... | collective-permute-start | bytes 1179656 | tf_op jit(solution)/shard_map/ppermute | solution.py:317
  14.8 16.6 %collective-permute-start.1 = (bf16[768,128]{1,0:T(8,128)(2,1)S(1)}, bf16[768,128]{1,0:T(8,128)(2,1)S(1)}, u32[]{:S(2)}, u32[]{:S(2)}) collective-permute-start(bf16[768,128]{1,0:T(8,128)(2,1)S(1)} %dynamic-slice_convert_fusion.refs_0_), channel_id=1, source_target_pairs={{0,2},{1,3},{2,0},{3,1},{4,6},{5,7},{6,4},{7,5},{8,10},{9,11},{10,... | collective-permute-start | bytes 589832 | tf_op jit(solution)/shard_map/ppermute | solution.py:331
  17.4 9.9 %collective-permute-start.3 = (bf16[384,256]{1,0:T(8,128)(2,1)S(1)}, bf16[384,256]{1,0:T(8,128)(2,1)S(1)}, u32[]{:S(2)}, u32[]{:S(2)}) collective-permute-start(bf16[384,256]{1,0:T(8,128)(2,1)S(1)} %get-tuple-element.35), channel_id=1, source_target_pairs={{0,2},{1,3},{2,0},{3,1},{4,6},{5,7},{6,4},{7,5},{8,10},{9,11},{10,... | collective-permute-start | bytes 589832 | tf_op jit(solution)/shard_map/ppermute | solution.py:347
  18.8 12.4 %collective-permute-start.9 = (bf16[384,256]{1,0:T(8,128)(2,1)S(1)}, bf16[384,256]{1,0:T(8,128)(2,1)S(1)}, u32[]{:S(2)}, u32[]{:S(2)}) collective-permute-start(bf16[384,256]{1,0:T(8,128)(2,1)S(1)} %get-tuple-element.33), channel_id=1, source_target_pairs={{0,2},{1,3},{2,0},{3,1},{4,6},{5,7},{6,4},{7,5},{8,10},{9,11},{10,... | collective-permute-start | bytes 589832 | tf_op jit(solution)/shard_map/ppermute | solution.py:347
  27.3 4.9 %collective-permute-start.4 = (bf16[384,256]{1,0:T(8,128)(2,1)S(1)}, bf16[384,256]{1,0:T(8,128)(2,1)S(1)}, u32[]{:S(2)}, u32[]{:S(2)}) collective-permute-start(bf16[384,256]{1,0:T(8,128)(2,1)S(1)} %add_convert_fusion.1.own_ref), channel_id=1, source_target_pairs={{0,1},{1,0},{2,3},{3,2},{4,5},{5,4},{6,7},{7,6},{8,9},{9,8},{10,11... | collective-permute-start | bytes 589832 | tf_op jit(solution)/shard_map/ppermute | solution.py:317
  31.3 5.9 %collective-permute-start.10 = (bf16[384,256]{1,0:T(8,128)(2,1)S(1)}, bf16[384,256]{1,0:T(8,128)(2,1)S(1)}, u32[]{:S(2)}, u32[]{:S(2)}) collective-permute-start(bf16[384,256]{1,0:T(8,128)(2,1)S(1)} %add_convert_fusion.own_ref), channel_id=1, source_target_pairs={{0,1},{1,0},{2,3},{3,2},{4,5},{5,4},{6,7},{7,6},{8,9},{9,8},{10,11... | collective-permute-start | bytes 589832 | tf_op jit(solution)/shard_map/ppermute | solution.py:317
  32.7 9.4 %collective-permute-start.5 = (bf16[128,256]{1,0:T(8,128)(2,1)S(1)}, bf16[128,256]{1,0:T(8,128)(2,1)S(1)}, u32[]{:S(2)}, u32[]{:S(2)}) collective-permute-start(bf16[128,256]{1,0:T(8,128)(2,1)S(1)} %get-tuple-element.24), channel_id=1, source_target_pairs={{0,4},{4,0},{8,12},{12,8},{1,5},{5,1},{9,13},{13,9},{2,6},{6,2},{1... | collective-permute-start | bytes 196616 | tf_op jit(solution)/shard_map/ppermute | solution.py:358
  34.6 7.5 %collective-permute-start.6 = (bf16[128,256]{1,0:T(8,128)(2,1)S(1)}, bf16[128,256]{1,0:T(8,128)(2,1)S(1)}, u32[]{:S(2)}, u32[]{:S(2)}) collective-permute-start(bf16[128,256]{1,0:T(8,128)(2,1)S(1)} %get-tuple-element.25), channel_id=1, source_target_pairs={{0,8},{4,12},{8,0},{12,4},{1,9},{5,13},{9,1},{13,5},{2,10},{6,14},... | collective-permute-start | bytes 196616 | tf_op jit(solution)/shard_map/ppermute | solution.py:358
  37.2 6.8 %collective-permute-start.7 = (bf16[128,256]{1,0:T(8,128)(2,1)S(1)}, bf16[128,256]{1,0:T(8,128)(2,1)S(1)}, u32[]{:S(2)}, u32[]{:S(2)}) collective-permute-start(bf16[128,256]{1,0:T(8,128)(2,1)S(1)} %get-tuple-element.26), channel_id=1, source_target_pairs={{0,12},{4,8},{8,4},{12,0},{1,13},{5,9},{9,5},{13,1},{2,14},{6,10},... | collective-permute-start | bytes 196616 | tf_op jit(solution)/shard_map/ppermute | solution.py:358
  37.6 6.3 %collective-permute-start.11 = (bf16[128,256]{1,0:T(8,128)(2,1)S(1)}, bf16[128,256]{1,0:T(8,128)(2,1)S(1)}, u32[]{:S(2)}, u32[]{:S(2)}) collective-permute-start(bf16[128,256]{1,0:T(8,128)(2,1)S(1)} %get-tuple-element.30), channel_id=1, source_target_pairs={{0,4},{4,0},{8,12},{12,8},{1,5},{5,1},{9,13},{13,9},{2,6},{6,2},{1... | collective-permute-start | bytes 196616 | tf_op jit(solution)/shard_map/ppermute | solution.py:358
  38.6 10.0 %collective-permute-start.12 = (bf16[128,256]{1,0:T(8,128)(2,1)S(1)}, bf16[128,256]{1,0:T(8,128)(2,1)S(1)}, u32[]{:S(2)}, u32[]{:S(2)}) collective-permute-start(bf16[128,256]{1,0:T(8,128)(2,1)S(1)} %get-tuple-element.31), channel_id=1, source_target_pairs={{0,8},{4,12},{8,0},{12,4},{1,9},{5,13},{9,1},{13,5},{2,10},{6,14},... | collective-permute-start | bytes 196616 | tf_op jit(solution)/shard_map/ppermute | solution.py:358
  42.1 6.5 %collective-permute-start.13 = (bf16[128,256]{1,0:T(8,128)(2,1)S(1)}, bf16[128,256]{1,0:T(8,128)(2,1)S(1)}, u32[]{:S(2)}, u32[]{:S(2)}) collective-permute-start(bf16[128,256]{1,0:T(8,128)(2,1)S(1)} %get-tuple-element.32), channel_id=1, source_target_pairs={{0,12},{4,8},{8,4},{12,0},{1,13},{5,9},{9,5},{13,1},{2,14},{6,10},... | collective-permute-start | bytes 196616 | tf_op jit(solution)/shard_map/ppermute | solution.py:358

commit v2 on v1

v2 whole, which is shorter than its diff:
```python
import functools

import jax
import jax.numpy as jnp
from jax import lax
from jax.experimental import pallas as pl
from jax.experimental.pallas import tpu as pltpu
from jax.sharding import PartitionSpec as P


CHUNKS = 2
TILE = 512
AHEAD = 8
MIB = 1 << 20


def partner_pairs(size):
    return [(i, i ^ 1) for i in range(size)]


def chip_shift(size, step):
    chips = size // 2
    return [(i, ((i // 2 + step) % chips) * 2 + i % 2) for i in range(size)]


def exchange(size, step):
    if size & (size - 1) == 0:
        return [(i, i ^ step) for i in range(size)]
    return [(i, (i + step) % size) for i in range(size)]


def receiver(size, me, step):
    return me ^ step if size & (size - 1) == 0 else (me + step) % size


def depth_tile(depth, most):
    tile = most // 128 * 128
    while depth % tile:
        tile -= 128
    return tile


def stream(far, near, far_w, near_w, sems):
    depth = near_w.shape[0]
    tile = depth_tile(depth, TILE)
    count = depth // tile

    def lines(t):
        return pl.ds(t * tile, tile)

    def copies(t):
        return (
            pltpu.make_async_copy(far_w.at[lines(t), :], near_w.at[lines(t), :], sems.at[0, t]),
            pltpu.make_async_copy(far.at[:, lines(t)], near.at[:, lines(t)], sems.at[1, t]),
        )

    def start(t):
        for copy in copies(t):
            copy.start()

    for t in range(min(AHEAD, count)):
        start(t)
    for t in range(count):
        for copy in copies(t):
            copy.wait()
        if t + AHEAD < count:
            start(t + AHEAD)
        yield lines(t), t == 0, t + 1 == count


def grads_kernel(chips, chip_ref, a_hbm, w_hbm, near_ref, *refs):
    far_refs, (a_ref, w_ref, total, sems) = refs[:-4], refs[-4:]
    for lines, begins, _ in stream(a_hbm, a_ref, w_hbm, w_ref, sems):
        product = jnp.dot(a_ref[:, lines], w_ref[lines, :], preferred_element_type=jnp.float32)
        if begins:
            total[...] = product
        else:
            total[...] += product
    width = near_ref.shape[1]
    for chip in range(chips):

        @pl.when(chip_ref[0] == chip)
        def _():
            near_ref[...] = total[:, pl.ds(chip * width, width)]
            for step, ref in enumerate(far_refs):
                place = (chip + step + 1) % chips * width
                ref[...] = total[:, pl.ds(place, width)].astype(ref.dtype)


def acts_kernel(core_ref, a_hbm, w_hbm, after_ref, *refs):
    halves, (a_ref, w_ref, total, sems) = refs[:-4], refs[-4:]
    half, width = halves[0].shape
    for lines, begins, ends in stream(a_hbm, a_ref, w_hbm, w_ref, sems):
        if not ends:
            product = jnp.dot(a_ref[:, lines], w_ref[lines, :], preferred_element_type=jnp.float32)
            if begins:
                total[...] = product
            else:
                total[...] += product
            continue
        for side in range(2):
            place = core_ref[0] if side == 0 else 1 - core_ref[0]
            rows = pl.ds(pl.multiple_of(place * half, half), half)
            result = jnp.dot(a_ref[rows, lines], w_ref[lines, :], preferred_element_type=jnp.float32)
            if not begins:
                result = total[rows, :] + result
            for chunk in range(len(halves) // 2):
                halves[2 * chunk + side][...] = result[:, chunk * width : (chunk + 1) * width]


def product_call(kernel, scalar, a, w, after, out):
    rows, depth = a.shape
    rank = w.shape[1]
    return pl.pallas_call(
        kernel,
        in_specs=[pl.BlockSpec(memory_space=pltpu.SMEM)]
        + [pl.BlockSpec(memory_space=pltpu.HBM)] * 2
        + [pl.BlockSpec(memory_space=pl.ANY)] * len(after),
        out_specs=[pl.BlockSpec(memory_space=pltpu.VMEM)] * len(out),
        out_shape=out,
        scratch_shapes=[
            pltpu.VMEM((rows, depth), a.dtype),
            pltpu.VMEM((depth, rank), w.dtype),
            pltpu.VMEM((rows, rank), jnp.float32),
            pltpu.SemaphoreType.DMA((2, depth // depth_tile(depth, TILE))),
        ],
        compiler_params=pltpu.CompilerParams(
            vmem_limit_bytes=2 * depth * (rows + rank) + 4 * rows * rank + 3 * MIB
        ),
        cost_estimate=pl.CostEstimate(
            flops=2 * rows * depth * rank,
            bytes_accessed=2 * (rows + rank) * depth,
            transcendentals=0,
        ),
    )(scalar, a, w, *after)


def project_grads(grads, proj_out, chip, chips):
    rows, rank = grads.shape[0], proj_out.shape[1]
    width = rank // chips
    out = [pltpu.VMEM((rows, width), jnp.float32)]
    out += [pltpu.VMEM((rows, width), jnp.bfloat16)] * (chips - 1)
    return product_call(functools.partial(grads_kernel, chips), chip, grads, proj_out, [], out)


def project_acts(acts, proj_in, core, after):
    rows, rank = acts.shape[0], proj_in.shape[1]
    out = [pltpu.VMEM((rows // 2, rank // CHUNKS), jnp.float32)] * (2 * CHUNKS)
    return product_call(acts_kernel, core, acts, proj_in, [after], out)


def vmem_call(kernel, scalars, arrays, out, limit=6, flops=10**5):
    arrays = [pltpu.with_memory_space_constraint(v, pltpu.VMEM) for v in arrays]
    return pl.pallas_call(
        kernel,
        in_specs=[pl.BlockSpec(memory_space=pltpu.SMEM)] * len(scalars)
        + [pl.BlockSpec(memory_space=pltpu.VMEM)] * len(arrays),
        out_specs=[pl.BlockSpec(memory_space=pltpu.VMEM)] * len(out),
        out_shape=out,
        compiler_params=pltpu.CompilerParams(vmem_limit_bytes=limit * MIB),
        cost_estimate=pl.CostEstimate(flops=flops, bytes_accessed=0, transcendentals=0),
    )(*scalars, *arrays)


def chip_sum_kernel(core_ref, near_ref, *refs):
    far_refs, (mine_ref, theirs_ref) = refs[:-2], refs[-2:]
    share = mine_ref.shape[1]
    for which in range(2):

        @pl.when(core_ref[0] == which)
        def _():
            for side, out_ref in ((which, mine_ref), (1 - which, theirs_ref)):
                place = pl.ds(side * share, share)
                total = near_ref[:, place]
                for ref in far_refs:
                    total = total + ref[:, place].astype(jnp.float32)
                out_ref[...] = total


def pair_sum_kernel(mine_ref, other_ref, total_ref, sent_ref):
    total = mine_ref[...] + other_ref[...]
    total_ref[...] = total
    sent_ref[...] = total.astype(sent_ref.dtype)


def spread_kernel(
    tok_count, core_ref, tok_ref, lengths_ref, owner_ref, mine_ref, other_ref, out_ref
):
    rows, share = mine_ref.shape
    docs = lengths_ref.shape[0]
    slots = docs // tok_count
    half = rows // 2
    tok, core = tok_ref[0], core_ref[0]
    starts, ends, targets = [], [], []
    seen = jnp.int32(0)
    for d in range(docs):
        starts.append(seen)
        seen = seen + lengths_ref[d]
        ends.append(seen)
        rank = jnp.int32(0)
        for e in range(d):
            rank = rank + (owner_ref[e] == owner_ref[d]).astype(jnp.int32)
        targets.append(owner_ref[d] * slots + rank)
    low = (mine_ref[...] + other_ref[...]).astype(jnp.bfloat16)
    turned = low.astype(jnp.float32).T
    for part in range(2):
        first = (core if part == 0 else 1 - core) * half
        position = tok * rows + first + lax.broadcasted_iota(jnp.int32, (share, half), 1)
        piece = jnp.where(
            core == part, turned[:, :half], turned[:, half:]
        )
        for step in range(tok_count):
            for slot in range(slots):
                want = receiver(tok_count, tok, step) * slots + slot
                begin = end = jnp.int32(0)
                for d in range(docs):
                    hit = targets[d] == want
                    begin = jnp.where(hit, starts[d], begin)
                    end = jnp.where(hit, ends[d], end)
                member = (position >= begin) & (position < end)
                out_ref[pl.ds((step * slots + slot) * share, share), pl.ds(part * half, half)] = (
                    jnp.where(member, piece, 0.0).astype(out_ref.dtype)
                )


def spread(mine, other, core, tok, doc_lengths, doc_owner, tok_count):
    rows, share = mine.shape
    out = pltpu.VMEM((doc_lengths.shape[0] * share, rows), jnp.bfloat16)
    (result,) = vmem_call(
        functools.partial(spread_kernel, tok_count),
        (core, tok, doc_lengths, doc_owner),
        (mine, other),
        [out],
        limit=8,
    )
    return result


def product_kernel(w_ref, own_ref, other_ref, kept_ref, *sent_refs):
    half = own_ref.shape[0]
    size = kept_ref.shape[0]
    product = jnp.dot(w_ref[:, :half], own_ref[...], preferred_element_type=jnp.float32)
    product += jnp.dot(w_ref[:, half:], other_ref[...], preferred_element_type=jnp.float32)
    kept_ref[...] = product[:size]
    for i, ref in enumerate(sent_refs):
        ref[...] = product[(i + 1) * size : (i + 2) * size].astype(ref.dtype)


def outer_products(spread_low, own, other, tok_count):
    size = spread_low.shape[0] // tok_count
    width = own.shape[1]
    return pl.pallas_call(
        product_kernel,
        in_specs=[pl.BlockSpec(memory_space=pltpu.VMEM)] * 3,
        out_specs=[pl.BlockSpec(memory_space=pltpu.VMEM)] * tok_count,
        out_shape=[pltpu.VMEM((size, width), jnp.float32)]
        + [pltpu.VMEM((size, width), jnp.bfloat16)] * (tok_count - 1),
        compiler_params=pltpu.CompilerParams(vmem_limit_bytes=6 * MIB),
        cost_estimate=pl.CostEstimate(
            flops=2 * spread_low.shape[0] * spread_low.shape[1] * width,
            bytes_accessed=0,
            transcendentals=0,
        ),
        name="outer_products",
    )(spread_low, own, other)


def finish_kernel(tok_count, tok_ref, lengths_ref, owner_ref, *refs):
    total_refs, out_ref = refs[:-1], refs[-1]
    docs = lengths_ref.shape[0]
    slots = docs // tok_count
    share = out_ref.shape[1]
    tok = tok_ref[0]
    for slot in range(slots):
        length = jnp.int32(0)
        for d in range(docs):
            rank = jnp.int32(0)
            for e in range(d):
                rank = rank + (owner_ref[e] == owner_ref[d]).astype(jnp.int32)
            hit = (owner_ref[d] == tok) & (rank == slot)
            length = jnp.where(hit, lengths_ref[d], length)
        place = 0
        for chunk in range(CHUNKS):
            parts = total_refs[chunk * tok_count : (chunk + 1) * tok_count]
            width = parts[0].shape[1]
            lines = pl.ds(slot * share, share)
            total = parts[0][lines, :]
            for part in parts[1:]:
                total = total + part[lines, :].astype(jnp.float32)
            scaling = lax.rsqrt(jnp.full((share, width), length, jnp.int32).astype(jnp.float32))
            out_ref[slot, :, pl.ds(place, width)] = total * scaling
            place += width


def finish(parts, tok, doc_lengths, doc_owner, tok_count, share):
    slots = doc_lengths.shape[0] // tok_count
    rank = sum(p.shape[1] for p in parts[::tok_count])
    return pl.pallas_call(
        functools.partial(finish_kernel, tok_count),
        in_specs=[pl.BlockSpec(memory_space=pltpu.SMEM)] * 3
        + [pl.BlockSpec(memory_space=pltpu.VMEM)] * len(parts),
        out_specs=pl.BlockSpec(memory_space=pltpu.VMEM),
        out_shape=jax.ShapeDtypeStruct((slots, share, rank), jnp.float32),
        compiler_params=pltpu.CompilerParams(vmem_limit_bytes=6 * MIB),
        name="finish",
    )(tok, doc_lengths, doc_owner, *parts)


def shards(acts, grads, proj_in, proj_out, doc_lengths, doc_owner):
    rank = proj_in.shape[1]
    tok_count = lax.axis_size("tok")
    feat_count = lax.axis_size("feat")
    chips = feat_count // 2
    feat = lax.axis_index("feat")
    chip = feat // 2
    core = (feat % 2).reshape(1)
    tok = lax.axis_index("tok").reshape(1)
    share = rank // feat_count
    rows = acts.shape[0]
    acts, grads, proj_in, proj_out = (
        pltpu.with_memory_space_constraint(v, pltpu.HBM) for v in (acts, grads, proj_in, proj_out)
    )

    def swap(value):
        return lax.ppermute(value, "feat", partner_pairs(feat_count))

    near, *far = project_grads(grads, proj_out, chip.reshape(1), chips)
    arrived = []
    for step in range(1, chips):
        arrived.append(lax.ppermute(far[step - 1], "feat", chip_shift(feat_count, step)))
    halves = project_acts(acts, proj_in, core, near)

    lows = []
    for chunk in range(CHUNKS):
        mine, theirs = halves[2 * chunk : 2 * chunk + 2]
        other = swap(theirs)
        full_in, sent = vmem_call(
            pair_sum_kernel,
            (),
            (mine, other),
            [pltpu.VMEM(mine.shape, jnp.float32), pltpu.VMEM(mine.shape, jnp.bfloat16)],
        )
        for step in range(1, chips):
            other = lax.ppermute(sent, "feat", chip_shift(feat_count, step))
            full_in = full_in + other.astype(jnp.float32)
        lows.append(full_in.astype(jnp.bfloat16))

    mine, theirs = vmem_call(
        chip_sum_kernel, (core,), (near, *arrived), [pltpu.VMEM((rows, share), jnp.float32)] * 2
    )
    other = swap(theirs)
    spread_low = spread(mine, other, core, tok, doc_lengths, doc_owner, tok_count)
    parts = []
    for low_in in lows:
        other = swap(low_in)
        kept, *sends = outer_products(spread_low, low_in, other, tok_count)
        parts.append(kept)
        for step in range(1, tok_count):
            parts.append(lax.ppermute(sends[step - 1], "tok", exchange(tok_count, step)))
    return finish(parts, tok, doc_lengths, doc_owner, tok_count, share)


def solution(mesh):
    in_specs = (
        P(("grp", "tok"), "feat"),
        P(("grp", "tok"), "feat"),
        P("feat", None),
        P("feat", None),
        P("grp"),
        P("grp"),
    )
    out_specs = P(("grp", "tok"), "feat", None)

    return jax.shard_map(shards, mesh=mesh, in_specs=in_specs, out_specs=out_specs, check_vma=False)
```

time: 50.1 us -> 51.6 us (1.030)
  waiting for transfers between devices: 18 us -> 20.5 us
  Pallas kernels: 16.4 us -> 14.7 us
  starting transfers between devices: 14.9 us -> 16.1 us
    ppermute x1, waiting for transfers between devices: 0.01 us -> 8.21 us  [shards(): lax.ppermute(far[step - 1], 'feat', chip_shift(feat_count, step))]
    ppermute x2, waiting for transfers between devices: 11.5 us -> 5.72 us  [shards(): other = lax.ppermute(sent, 'feat', chip_shift(feat_count, step))]
    pallas_call x4 -> x6, Pallas kernels: 14.2 us -> 12.6 us  [the longest x2 11.6 us: product_call(): pl.pallas_call(kernel, in_specs=[pl.BlockSpec(memory_space=pltpu.SMEM)] +...]
    ppermute x2, starting transfers between devices: 2.15 us -> 3.64 us  [shards(): other = lax.ppermute(sent, 'feat', chip_shift(feat_count, step))]
  transfers between devices with their start and end apart: 14 -> 14, of which waited for: 4 -> 5; matrix products, arithmetic and copies ran while one was open for 1% -> 0% of each run, Pallas kernels for 10% -> 4%
where the time goes in v2:
time: 51.6 us; the launch traced here: 51.5 us
  waiting for transfers between devices  20.5 us (40%)
  starting transfers between devices  16.1 us (31%)
  Pallas kernels  14.7 us (28%)
    pallas_call x2, Pallas kernels, product_call(): pl.pallas_call(kernel, in_specs=[pl.BlockSpec(memory_space=pltpu.SMEM)] +...  11.6 us
    ppermute x6, starting transfers between devices, shards(): lax.ppermute(sends[step - 1], 'tok', exchange(tok_count, step))  8.91 us
    ppermute x1, waiting for transfers between devices, shards(): lax.ppermute(far[step - 1], 'feat', chip_shift(feat_count, step))  8.21 us
    ppermute x6, waiting for transfers between devices, shards(): lax.ppermute(sends[step - 1], 'tok', exchange(tok_count, step))  6.53 us
    ppermute x2, waiting for transfers between devices, shards(): other = lax.ppermute(sent, 'feat', chip_shift(feat_count, step))  5.72 us
    ppermute x2, starting transfers between devices, shards(): other = lax.ppermute(sent, 'feat', chip_shift(feat_count, step))  3.64 us
    ppermute x1, starting transfers between devices, shards(): lax.ppermute(far[step - 1], 'feat', chip_shift(feat_count, step))  2.58 us
    pallas_call x1, Pallas kernels, finish(): pl.pallas_call(functools.partial(finish_kernel, tok_count), in_specs=[pl....  1.31 us
  transfers between devices with their start and end apart: 14, of which 5 were waited for; matrix products, arithmetic and copies ran while one was open for 0% of the time, Pallas kernels for 4%

profile of v2, /device:TPU:0, one launch (start us, length us, event | category | flops | bytes accessed | tf_op | source)
XLA Modules:
  0.0 51.5 jit_solution(4369806186355750795)
XLA Ops:
  0.0 3.4 %shard_map.64 = (f32[768,256]{1,0:T(8,128)S(1)}, bf16[768,256]{1,0:T(8,128)(2,1)S(1)}) custom-call(s32[1]{0:T(128)} %bitcast.2.chip_ref, bf16[768,2048]{1,0:T(8,128)(2,1)} %a_hbm.2, bf16[2048,512]{1,0:T(8,128)(2,1)} %w_hbm.2), custom_call_target="tpu_custom_call" | custom-call | flops 1610612736 | bytes 5242880 | tf_op jit(solution)/shard_map/pallas_call | solution.py:114
  3.4 0.0 copy-start
  3.4 0.0 copy-start.1
  3.4 8.2 %shard_map.67 = (f32[384,256]{1,0:T(8,128)S(1)}, f32[384,256]{1,0:T(8,128)S(1)}, f32[384,256]{1,0:T(8,128)S(1)}, f32[384,256]{1,0:T(8,128)S(1)}) custom-call(s32[1]{0:T(128)} %bitcast.1.core_ref, bf16[768,7168]{1,0:T(8,128)(2,1)} %a_hbm.3, bf16[7168,512]{1,0:T(8,128)(2,1)} %w_hbm.3, f32[768,256]{1,0:T(8,128)S(1)} %get-tuple-element.25.near_ref.after_ref), custom_call_target="tpu_custom_call" | custom-call | flops 5637144576 | bytes 18350080 | tf_op jit(solution)/shard_map/pallas_call | solution.py:114
  11.6 0.6 %collective-permute-start.2 = (f32[384,256]{1,0:T(8,128)S(1)}, f32[384,256]{1,0:T(8,128)S(1)}, u32[]{:S(2)}, u32[]{:S(2)}) collective-permute-start(f32[384,256]{1,0:T(8,128)S(1)} %get-tuple-element.30), channel_id=1, source_target_pairs={{0,1},{1,0},{2,3},{3,2},{4,5},{5,4},{6,7},{7,6},{8,9},{9,8},{10,11... | collective-permute-start | bytes 1179656 | tf_op jit(solution)/shard_map/ppermute | solution.py:325
  12.2 2.6 %collective-permute-start = (bf16[768,256]{1,0:T(8,128)(2,1)S(1)}, bf16[768,256]{1,0:T(8,128)(2,1)S(1)}, u32[]{:S(2)}, u32[]{:S(2)}) collective-permute-start(bf16[768,256]{1,0:T(8,128)(2,1)S(1)} %get-tuple-element.26), channel_id=1, source_target_pairs={{0,2},{1,3},{2,0},{3,1},{4,6},{5,7},{6,4},{7,5},{8,10},{9,11},{10,... | collective-permute-start | bytes 1179656 | tf_op jit(solution)/shard_map/ppermute | solution.py:330
  14.8 0.2 collective-permute-start.8
  14.9 0.0 collective-permute-done.2.other_ref
  15.0 1.6 %collective-permute-start.3 = (bf16[384,256]{1,0:T(8,128)(2,1)S(1)}, bf16[384,256]{1,0:T(8,128)(2,1)S(1)}, u32[]{:S(2)}, u32[]{:S(2)}) collective-permute-start(bf16[384,256]{1,0:T(8,128)(2,1)S(1)} %get-tuple-element.32), channel_id=1, source_target_pairs={{0,2},{1,3},{2,0},{3,1},{4,6},{5,7},{6,4},{7,5},{8,10},{9,11},{10,... | collective-permute-start | bytes 589832 | tf_op jit(solution)/shard_map/ppermute | solution.py:344
  16.5 8.2 %collective-permute-done.refs_0_ = bf16[768,256]{1,0:T(8,128)(2,1)S(1)} collective-permute-done((bf16[768,256]{1,0:T(8,128)(2,1)S(1)}, bf16[768,256]{1,0:T(8,128)(2,1)S(1)}, u32[]{:S(2)}, u32[]{:S(2)}) %collective-permute-start) | collective-permute-done | bytes 393248 | tf_op jit(solution)/shard_map/ppermute | solution.py:330
  24.7 0.1 shard_map.65
  24.8 0.1 collective-permute-start.1
  24.9 0.0 collective-permute-done.8.other_ref
  25.0 2.1 %collective-permute-start.9 = (bf16[384,256]{1,0:T(8,128)(2,1)S(1)}, bf16[384,256]{1,0:T(8,128)(2,1)S(1)}, u32[]{:S(2)}, u32[]{:S(2)}) collective-permute-start(bf16[384,256]{1,0:T(8,128)(2,1)S(1)} %get-tuple-element.40), channel_id=1, source_target_pairs={{0,2},{1,3},{2,0},{3,1},{4,6},{5,7},{6,4},{7,5},{8,10},{9,11},{10,... | collective-permute-start | bytes 589832 | tf_op jit(solution)/shard_map/ppermute | solution.py:344
  27.1 1.9 %collective-permute-done.3 = bf16[384,256]{1,0:T(8,128)(2,1)S(1)} collective-permute-done((bf16[384,256]{1,0:T(8,128)(2,1)S(1)}, bf16[384,256]{1,0:T(8,128)(2,1)S(1)}, u32[]{:S(2)}, u32[]{:S(2)}) %collective-permute-start.3) | collective-permute-done | bytes 196640 | tf_op jit(solution)/shard_map/ppermute | solution.py:344
  29.0 0.1 collective-permute-start.4
  29.1 3.8 %collective-permute-done.9 = bf16[384,256]{1,0:T(8,128)(2,1)S(1)} collective-permute-done((bf16[384,256]{1,0:T(8,128)(2,1)S(1)}, bf16[384,256]{1,0:T(8,128)(2,1)S(1)}, u32[]{:S(2)}, u32[]{:S(2)}) %collective-permute-start.9) | collective-permute-done | bytes 196640 | tf_op jit(solution)/shard_map/ppermute | solution.py:344
  33.0 0.1 collective-permute-start.10
  33.0 0.0 collective-permute-done.1.other_ref
  33.1 0.0 copy-done
  33.1 0.0 copy-done.1
  33.1 0.8 %shard_map.66.w_ref = bf16[512,768]{1,0:T(8,128)(2,1)S(1)} custom-call(s32[1]{0:T(128)} %bitcast.1.core_ref, s32[1]{0:T(128)} %bitcast.tok_ref, s32[4]{0:T(128)S(1)} %copy-done, s32[4]{0:T(128)S(1)} %copy-done.1, f32[768,128]{1,0:T(8,128)S(1)} %get-tuple-element.27.mine_ref, f32[768,128]{1,0:T(8,128)S(1)} %collective-permute-done.1.other_ref), custom_call_target="tpu_custom_call" | custom-call | flops 100000 | tf_op jit(solution)/shard_map/pallas_call | solution.py:154
  33.9 0.0 collective-permute-done.4.other_ref
  33.9 0.4 outer_products.2
  34.3 1.9 %collective-permute-start.5 = (bf16[128,256]{1,0:T(8,128)(2,1)S(1)}, bf16[128,256]{1,0:T(8,128)(2,1)S(1)}, u32[]{:S(2)}, u32[]{:S(2)}) collective-permute-start(bf16[128,256]{1,0:T(8,128)(2,1)S(1)} %get-tuple-element.34), channel_id=1, source_target_pairs={{0,4},{4,0},{8,12},{12,8},{1,5},{5,1},{9,13},{13,9},{2,6},{6,2},{1... | collective-permute-start | bytes 196616 | tf_op jit(solution)/shard_map/ppermute | solution.py:359
  36.2 2.6 %collective-permute-start.6 = (bf16[128,256]{1,0:T(8,128)(2,1)S(1)}, bf16[128,256]{1,0:T(8,128)(2,1)S(1)}, u32[]{:S(2)}, u32[]{:S(2)}) collective-permute-start(bf16[128,256]{1,0:T(8,128)(2,1)S(1)} %get-tuple-element.35), channel_id=1, source_target_pairs={{0,8},{4,12},{8,0},{12,4},{1,9},{5,13},{9,1},{13,5},{2,10},{6,14},... | collective-permute-start | bytes 196616 | tf_op jit(solution)/shard_map/ppermute | solution.py:359
  38.8 0.0 collective-permute-start.7
  38.8 0.0 collective-permute-done.10.other_ref
  38.8 0.4 outer_products.3
  39.2 1.0 %collective-permute-start.11 = (bf16[128,256]{1,0:T(8,128)(2,1)S(1)}, bf16[128,256]{1,0:T(8,128)(2,1)S(1)}, u32[]{:S(2)}, u32[]{:S(2)}) collective-permute-start(bf16[128,256]{1,0:T(8,128)(2,1)S(1)} %get-tuple-element.42), channel_id=1, source_target_pairs={{0,4},{4,0},{8,12},{12,8},{1,5},{5,1},{9,13},{13,9},{2,6},{6,2},{1... | collective-permute-start | bytes 196616 | tf_op jit(solution)/shard_map/ppermute | solution.py:359
  40.2 3.5 %collective-permute-start.12 = (bf16[128,256]{1,0:T(8,128)(2,1)S(1)}, bf16[128,256]{1,0:T(8,128)(2,1)S(1)}, u32[]{:S(2)}, u32[]{:S(2)}) collective-permute-start(bf16[128,256]{1,0:T(8,128)(2,1)S(1)} %get-tuple-element.43), channel_id=1, source_target_pairs={{0,8},{4,12},{8,0},{12,4},{1,9},{5,13},{9,1},{13,5},{2,10},{6,14},... | collective-permute-start | bytes 196616 | tf_op jit(solution)/shard_map/ppermute | solution.py:359
  43.6 0.0 collective-permute-done.5.refs_1_
  43.6 0.0 collective-permute-start.13
  43.6 0.0 collective-permute-done.6.refs_2_
  43.7 1.9 %collective-permute-done.7.refs_3_ = bf16[128,256]{1,0:T(8,128)(2,1)S(1)} collective-permute-done((bf16[128,256]{1,0:T(8,128)(2,1)S(1)}, bf16[128,256]{1,0:T(8,128)(2,1)S(1)}, u32[]{:S(2)}, u32[]{:S(2)}) %collective-permute-start.7) | collective-permute-done | bytes 65568 | tf_op jit(solution)/shard_map/ppermute | solution.py:359
  45.5 0.0 collective-permute-done.11.refs_5_
  45.5 4.7 %collective-permute-done.12.refs_6_ = bf16[128,256]{1,0:T(8,128)(2,1)S(1)} collective-permute-done((bf16[128,256]{1,0:T(8,128)(2,1)S(1)}, bf16[128,256]{1,0:T(8,128)(2,1)S(1)}, u32[]{:S(2)}, u32[]{:S(2)}) %collective-permute-start.12) | collective-permute-done | bytes 65568 | tf_op jit(solution)/shard_map/ppermute | solution.py:359
  50.2 0.0 collective-permute-done.13.refs_7_
  50.2 1.3 %finish.1 = f32[1,128,512]{2,1,0:T(8,128)} custom-call(s32[1]{0:T(128)} %bitcast.tok_ref, s32[4]{0:T(128)S(1)} %copy-done, s32[4]{0:T(128)S(1)} %copy-done.1, f32[128,256]{1,0:T(8,128)S(1)} %get-tuple-element.33.refs_0_, bf16[128,256]{1,0:T(8,128)(2,1)S(1)} %collective-permute-done.5.refs_1_, bf16[128,256]{1,0:T(8,128)(2,1)S(1)} %collective-permute-done.6.refs_2_, ...), custom_call_target="tpu_custom_call" | custom-call | tf_op jit(solution)/shard_map/finish/pallas_call | solution.py:298
  (4 shorter events, 0.2 us)
Async XLA Ops:
  3.4 29.7 %copy-start = (s32[4]{0:T(128)S(1)}, s32[4]{0:T(128)}, u32[]{:S(2)}) copy-start(s32[4]{0:T(128)} %lengths_ref.3) | copy-start | bytes 52
  3.4 29.7 %copy-start.1 = (s32[4]{0:T(128)S(1)}, s32[4]{0:T(128)}, u32[]{:S(2)}) copy-start(s32[4]{0:T(128)} %owner_ref.3) | copy-start | bytes 52
  11.6 3.3 %collective-permute-start.2 = (f32[384,256]{1,0:T(8,128)S(1)}, f32[384,256]{1,0:T(8,128)S(1)}, u32[]{:S(2)}, u32[]{:S(2)}) collective-permute-start(f32[384,256]{1,0:T(8,128)S(1)} %get-tuple-element.30), channel_id=1, source_target_pairs={{0,1},{1,0},{2,3},{3,2},{4,5},{5,4},{6,7},{7,6},{8,9},{9,8},{10,11... | collective-permute-start | bytes 1179656 | tf_op jit(solution)/shard_map/ppermute | solution.py:325
  12.2 12.5 %collective-permute-start = (bf16[768,256]{1,0:T(8,128)(2,1)S(1)}, bf16[768,256]{1,0:T(8,128)(2,1)S(1)}, u32[]{:S(2)}, u32[]{:S(2)}) collective-permute-start(bf16[768,256]{1,0:T(8,128)(2,1)S(1)} %get-tuple-element.26), channel_id=1, source_target_pairs={{0,2},{1,3},{2,0},{3,1},{4,6},{5,7},{6,4},{7,5},{8,10},{9,11},{10,... | collective-permute-start | bytes 1179656 | tf_op jit(solution)/shard_map/ppermute | solution.py:330
  14.8 10.1 %collective-permute-start.8 = (f32[384,256]{1,0:T(8,128)S(1)}, f32[384,256]{1,0:T(8,128)S(1)}, u32[]{:S(2)}, u32[]{:S(2)}) collective-permute-start(f32[384,256]{1,0:T(8,128)S(1)} %get-tuple-element.38), channel_id=1, source_target_pairs={{0,1},{1,0},{2,3},{3,2},{4,5},{5,4},{6,7},{7,6},{8,9},{9,8},{10,11... | collective-permute-start | bytes 1179656 | tf_op jit(solution)/shard_map/ppermute | solution.py:325
  15.0 14.0 %collective-permute-start.3 = (bf16[384,256]{1,0:T(8,128)(2,1)S(1)}, bf16[384,256]{1,0:T(8,128)(2,1)S(1)}, u32[]{:S(2)}, u32[]{:S(2)}) collective-permute-start(bf16[384,256]{1,0:T(8,128)(2,1)S(1)} %get-tuple-element.32), channel_id=1, source_target_pairs={{0,2},{1,3},{2,0},{3,1},{4,6},{5,7},{6,4},{7,5},{8,10},{9,11},{10,... | collective-permute-start | bytes 589832 | tf_op jit(solution)/shard_map/ppermute | solution.py:344
  24.8 8.2 %collective-permute-start.1 = (f32[768,128]{1,0:T(8,128)S(1)}, f32[768,128]{1,0:T(8,128)S(1)}, u32[]{:S(2)}, u32[]{:S(2)}) collective-permute-start(f32[768,128]{1,0:T(8,128)S(1)} %get-tuple-element.28), channel_id=1, source_target_pairs={{0,1},{1,0},{2,3},{3,2},{4,5},{5,4},{6,7},{7,6},{8,9},{9,8},{10,11... | collective-permute-start | bytes 1179656 | tf_op jit(solution)/shard_map/ppermute | solution.py:325
  25.0 7.9 %collective-permute-start.9 = (bf16[384,256]{1,0:T(8,128)(2,1)S(1)}, bf16[384,256]{1,0:T(8,128)(2,1)S(1)}, u32[]{:S(2)}, u32[]{:S(2)}) collective-permute-start(bf16[384,256]{1,0:T(8,128)(2,1)S(1)} %get-tuple-element.40), channel_id=1, source_target_pairs={{0,2},{1,3},{2,0},{3,1},{4,6},{5,7},{6,4},{7,5},{8,10},{9,11},{10,... | collective-permute-start | bytes 589832 | tf_op jit(solution)/shard_map/ppermute | solution.py:344
  29.0 4.9 %collective-permute-start.4 = (bf16[384,256]{1,0:T(8,128)(2,1)S(1)}, bf16[384,256]{1,0:T(8,128)(2,1)S(1)}, u32[]{:S(2)}, u32[]{:S(2)}) collective-permute-start(bf16[384,256]{1,0:T(8,128)(2,1)S(1)} %add_convert_fusion.1.own_ref), channel_id=1, source_target_pairs={{0,1},{1,0},{2,3},{3,2},{4,5},{5,4},{6,7},{7,6},{8,9},{9,8},{10,11... | collective-permute-start | bytes 589832 | tf_op jit(solution)/shard_map/ppermute | solution.py:325
  33.0 5.8 %collective-permute-start.10 = (bf16[384,256]{1,0:T(8,128)(2,1)S(1)}, bf16[384,256]{1,0:T(8,128)(2,1)S(1)}, u32[]{:S(2)}, u32[]{:S(2)}) collective-permute-start(bf16[384,256]{1,0:T(8,128)(2,1)S(1)} %add_convert_fusion.own_ref), channel_id=1, source_target_pairs={{0,1},{1,0},{2,3},{3,2},{4,5},{5,4},{6,7},{7,6},{8,9},{9,8},{10,11... | collective-permute-start | bytes 589832 | tf_op jit(solution)/shard_map/ppermute | solution.py:325
  34.3 9.3 %collective-permute-start.5 = (bf16[128,256]{1,0:T(8,128)(2,1)S(1)}, bf16[128,256]{1,0:T(8,128)(2,1)S(1)}, u32[]{:S(2)}, u32[]{:S(2)}) collective-permute-start(bf16[128,256]{1,0:T(8,128)(2,1)S(1)} %get-tuple-element.34), channel_id=1, source_target_pairs={{0,4},{4,0},{8,12},{12,8},{1,5},{5,1},{9,13},{13,9},{2,6},{6,2},{1... | collective-permute-start | bytes 196616 | tf_op jit(solution)/shard_map/ppermute | solution.py:359
  36.2 7.5 %collective-permute-start.6 = (bf16[128,256]{1,0:T(8,128)(2,1)S(1)}, bf16[128,256]{1,0:T(8,128)(2,1)S(1)}, u32[]{:S(2)}, u32[]{:S(2)}) collective-permute-start(bf16[128,256]{1,0:T(8,128)(2,1)S(1)} %get-tuple-element.35), channel_id=1, source_target_pairs={{0,8},{4,12},{8,0},{12,4},{1,9},{5,13},{9,1},{13,5},{2,10},{6,14},... | collective-permute-start | bytes 196616 | tf_op jit(solution)/shard_map/ppermute | solution.py:359
  38.8 6.8 %collective-permute-start.7 = (bf16[128,256]{1,0:T(8,128)(2,1)S(1)}, bf16[128,256]{1,0:T(8,128)(2,1)S(1)}, u32[]{:S(2)}, u32[]{:S(2)}) collective-permute-start(bf16[128,256]{1,0:T(8,128)(2,1)S(1)} %get-tuple-element.36), channel_id=1, source_target_pairs={{0,12},{4,8},{8,4},{12,0},{1,13},{5,9},{9,5},{13,1},{2,14},{6,10},... | collective-permute-start | bytes 196616 | tf_op jit(solution)/shard_map/ppermute | solution.py:359
  39.2 6.3 %collective-permute-start.11 = (bf16[128,256]{1,0:T(8,128)(2,1)S(1)}, bf16[128,256]{1,0:T(8,128)(2,1)S(1)}, u32[]{:S(2)}, u32[]{:S(2)}) collective-permute-start(bf16[128,256]{1,0:T(8,128)(2,1)S(1)} %get-tuple-element.42), channel_id=1, source_target_pairs={{0,4},{4,0},{8,12},{12,8},{1,5},{5,1},{9,13},{13,9},{2,6},{6,2},{1... | collective-permute-start | bytes 196616 | tf_op jit(solution)/shard_map/ppermute | solution.py:359
  40.2 10.0 %collective-permute-start.12 = (bf16[128,256]{1,0:T(8,128)(2,1)S(1)}, bf16[128,256]{1,0:T(8,128)(2,1)S(1)}, u32[]{:S(2)}, u32[]{:S(2)}) collective-permute-start(bf16[128,256]{1,0:T(8,128)(2,1)S(1)} %get-tuple-element.43), channel_id=1, source_target_pairs={{0,8},{4,12},{8,0},{12,4},{1,9},{5,13},{9,1},{13,5},{2,10},{6,14},... | collective-permute-start | bytes 196616 | tf_op jit(solution)/shard_map/ppermute | solution.py:359
  43.6 6.5 %collective-permute-start.13 = (bf16[128,256]{1,0:T(8,128)(2,1)S(1)}, bf16[128,256]{1,0:T(8,128)(2,1)S(1)}, u32[]{:S(2)}, u32[]{:S(2)}) collective-permute-start(bf16[128,256]{1,0:T(8,128)(2,1)S(1)} %get-tuple-element.44), channel_id=1, source_target_pairs={{0,12},{4,8},{8,4},{12,0},{1,13},{5,9},{9,5},{13,1},{2,14},{6,10},... | collective-permute-start | bytes 196616 | tf_op jit(solution)/shard_map/ppermute | solution.py:359

commit v3 on v2

--- a/solution.py
+++ b/solution.py
@@ -184,7 +184,7 @@
 
 
 def spread_kernel(
-    tok_count, core_ref, tok_ref, lengths_ref, owner_ref, mine_ref, other_ref, out_ref
+    tok_count, core_ref, tok_ref, lengths_ref, owner_ref, mine_ref, other_ref, out_ref, scale_ref
 ):
     rows, share = mine_ref.shape
     docs = lengths_ref.shape[0]
@@ -201,6 +201,12 @@
         for e in range(d):
             rank = rank + (owner_ref[e] == owner_ref[d]).astype(jnp.int32)
         targets.append(owner_ref[d] * slots + rank)
+    for slot in range(slots):
+        length = jnp.int32(1)
+        for d in range(docs):
+            length = jnp.where(targets[d] == tok * slots + slot, lengths_ref[d], length)
+        length = jnp.full((8, 128), length, jnp.int32).astype(jnp.float32)
+        scale_ref[pl.ds(slot * 8, 8), :] = lax.rsqrt(length)
     low = (mine_ref[...] + other_ref[...]).astype(jnp.bfloat16)
     turned = low.astype(jnp.float32).T
     for part in range(2):
@@ -225,15 +231,17 @@
 
 def spread(mine, other, core, tok, doc_lengths, doc_owner, tok_count):
     rows, share = mine.shape
-    out = pltpu.VMEM((doc_lengths.shape[0] * share, rows), jnp.bfloat16)
-    (result,) = vmem_call(
+    docs = doc_lengths.shape[0]
+    return vmem_call(
         functools.partial(spread_kernel, tok_count),
         (core, tok, doc_lengths, doc_owner),
         (mine, other),
-        [out],
+        [
+            pltpu.VMEM((docs * share, rows), jnp.bfloat16),
+            pltpu.VMEM((docs // tok_count * 8, 128), jnp.float32),
+        ],
         limit=8,
     )
-    return result
 
 
 def product_kernel(w_ref, own_ref, other_ref, kept_ref, *sent_refs):
@@ -265,45 +273,29 @@
     )(spread_low, own, other)
 
 
-def finish_kernel(tok_count, tok_ref, lengths_ref, owner_ref, *refs):
+def finish_kernel(tok_count, scale_ref, *refs):
     total_refs, out_ref = refs[:-1], refs[-1]
-    docs = lengths_ref.shape[0]
-    slots = docs // tok_count
-    share = out_ref.shape[1]
-    tok = tok_ref[0]
+    slots, share, _ = out_ref.shape
     for slot in range(slots):
-        length = jnp.int32(0)
-        for d in range(docs):
-            rank = jnp.int32(0)
-            for e in range(d):
-                rank = rank + (owner_ref[e] == owner_ref[d]).astype(jnp.int32)
-            hit = (owner_ref[d] == tok) & (rank == slot)
-            length = jnp.where(hit, lengths_ref[d], length)
+        scale = jnp.broadcast_to(scale_ref[pl.ds(slot * 8, 1), :], (share, 128))
+        lines = pl.ds(slot * share, share)
         place = 0
         for chunk in range(CHUNKS):
             parts = total_refs[chunk * tok_count : (chunk + 1) * tok_count]
-            width = parts[0].shape[1]
-            lines = pl.ds(slot * share, share)
-            total = parts[0][lines, :]
-            for part in parts[1:]:
-                total = total + part[lines, :].astype(jnp.float32)
-            scaling = lax.rsqrt(jnp.full((share, width), length, jnp.int32).astype(jnp.float32))
-            out_ref[slot, :, pl.ds(place, width)] = total * scaling
-            place += width
-
-
-def finish(parts, tok, doc_lengths, doc_owner, tok_count, share):
-    slots = doc_lengths.shape[0] // tok_count
+            for begin in range(0, parts[0].shape[1], 128):
+                columns = pl.ds(begin, 128)
+                total = parts[0][lines, columns]
+                for part in parts[1:]:
+                    total = total + part[lines, columns].astype(jnp.float32)
+                out_ref[slot, :, pl.ds(place, 128)] = total * scale
+                place += 128
+
+
+def finish(parts, scale, tok_count, slots, share):
     rank = sum(p.shape[1] for p in parts[::tok_count])
-    return pl.pallas_call(
-        functools.partial(finish_kernel, tok_count),
-        in_specs=[pl.BlockSpec(memory_space=pltpu.SMEM)] * 3
-        + [pl.BlockSpec(memory_space=pltpu.VMEM)] * len(parts),
-        out_specs=pl.BlockSpec(memory_space=pltpu.VMEM),
-        out_shape=jax.ShapeDtypeStruct((slots, share, rank), jnp.float32),
-        compiler_params=pltpu.CompilerParams(vmem_limit_bytes=6 * MIB),
-        name="finish",
-    )(tok, doc_lengths, doc_owner, *parts)
+    out = [jax.ShapeDtypeStruct((slots, share, rank), jnp.float32)]
+    (result,) = vmem_call(functools.partial(finish_kernel, tok_count), (), (scale, *parts), out)
+    return result
 
 
 def shards(acts, grads, proj_in, proj_out, doc_lengths, doc_owner):
@@ -349,7 +341,7 @@
         chip_sum_kernel, (core,), (near, *arrived), [pltpu.VMEM((rows, share), jnp.float32)] * 2
     )
     other = swap(theirs)
-    spread_low = spread(mine, other, core, tok, doc_lengths, doc_owner, tok_count)
+    spread_low, scale = spread(mine, other, core, tok, doc_lengths, doc_owner, tok_count)
     parts = []
     for low_in in lows:
         other = swap(low_in)
@@ -357,7 +349,7 @@
         parts.append(kept)
         for step in range(1, tok_count):
             parts.append(lax.ppermute(sends[step - 1], "tok", exchange(tok_count, step)))
-    return finish(parts, tok, doc_lengths, doc_owner, tok_count, share)
+    return finish(parts, scale, tok_count, doc_lengths.shape[0] // tok_count, share)
 
 
 def solution(mesh):

time: 51.6 us -> 51.1 us (level)
    pallas_call x1 -> x0, Pallas kernels: 1.31 us -> none  [finish(): pl.pallas_call(functools.partial(finish_kernel, tok_count), in_specs=[pl....]
    pallas_call x4 -> x5, Pallas kernels: 0.96 us -> 1.73 us  [vmem_call(): pl.pallas_call(kernel, in_specs=[pl.BlockSpec(memory_space=pltpu.SMEM)] *...]
where the time goes in v3:
time: 51.1 us; the launch traced here: 50.9 us
  waiting for transfers between devices  20.5 us (40%)
  starting transfers between devices  16.1 us (32%)
  Pallas kernels  14.2 us (28%)
    pallas_call x2, Pallas kernels, product_call(): pl.pallas_call(kernel, in_specs=[pl.BlockSpec(memory_space=pltpu.SMEM)] +...  11.6 us
    ppermute x6, starting transfers between devices, shards(): lax.ppermute(sends[step - 1], 'tok', exchange(tok_count, step))  8.91 us
    ppermute x1, waiting for transfers between devices, shards(): lax.ppermute(far[step - 1], 'feat', chip_shift(feat_count, step))  8.21 us
    ppermute x6, waiting for transfers between devices, shards(): lax.ppermute(sends[step - 1], 'tok', exchange(tok_count, step))  6.53 us
    ppermute x2, waiting for transfers between devices, shards(): other = lax.ppermute(sent, 'feat', chip_shift(feat_count, step))  5.72 us
    ppermute x2, starting transfers between devices, shards(): other = lax.ppermute(sent, 'feat', chip_shift(feat_count, step))  3.64 us
    ppermute x1, starting transfers between devices, shards(): lax.ppermute(far[step - 1], 'feat', chip_shift(feat_count, step))  2.58 us
    pallas_call x5, Pallas kernels, vmem_call(): pl.pallas_call(kernel, in_specs=[pl.BlockSpec(memory_space=pltpu.SMEM)] *...  1.73 us
  transfers between devices with their start and end apart: 14, of which 5 were waited for; matrix products, arithmetic and copies ran while one was open for 0% of the time, Pallas kernels for 4%

profile of v3, /device:TPU:0, one launch (start us, length us, event | category | flops | bytes accessed | tf_op | source)
XLA Modules:
  0.0 50.9 jit_solution(5960875457926650462)
XLA Ops:
  0.0 3.4 %shard_map.64 = (f32[768,256]{1,0:T(8,128)S(1)}, bf16[768,256]{1,0:T(8,128)(2,1)S(1)}) custom-call(s32[1]{0:T(128)} %bitcast.2.chip_ref, bf16[768,2048]{1,0:T(8,128)(2,1)} %a_hbm.2, bf16[2048,512]{1,0:T(8,128)(2,1)} %w_hbm.2), custom_call_target="tpu_custom_call" | custom-call | flops 1610612736 | bytes 5242880 | tf_op jit(solution)/shard_map/pallas_call | solution.py:114
  3.4 0.0 copy-start
  3.4 0.0 copy-start.1
  3.4 8.2 %shard_map.67 = (f32[384,256]{1,0:T(8,128)S(1)}, f32[384,256]{1,0:T(8,128)S(1)}, f32[384,256]{1,0:T(8,128)S(1)}, f32[384,256]{1,0:T(8,128)S(1)}) custom-call(s32[1]{0:T(128)} %bitcast.core_ref, bf16[768,7168]{1,0:T(8,128)(2,1)} %a_hbm.3, bf16[7168,512]{1,0:T(8,128)(2,1)} %w_hbm.3, f32[768,256]{1,0:T(8,128)S(1)} %get-tuple-element.27.near_ref.after_ref), custom_call_target="tpu_custom_call" | custom-call | flops 5637144576 | bytes 18350080 | tf_op jit(solution)/shard_map/pallas_call | solution.py:114
  11.6 0.6 %collective-permute-start.2 = (f32[384,256]{1,0:T(8,128)S(1)}, f32[384,256]{1,0:T(8,128)S(1)}, u32[]{:S(2)}, u32[]{:S(2)}) collective-permute-start(f32[384,256]{1,0:T(8,128)S(1)} %get-tuple-element.34), channel_id=1, source_target_pairs={{0,1},{1,0},{2,3},{3,2},{4,5},{5,4},{6,7},{7,6},{8,9},{9,8},{10,11... | collective-permute-start | bytes 1179656 | tf_op jit(solution)/shard_map/ppermute | solution.py:317
  12.2 2.6 %collective-permute-start = (bf16[768,256]{1,0:T(8,128)(2,1)S(1)}, bf16[768,256]{1,0:T(8,128)(2,1)S(1)}, u32[]{:S(2)}, u32[]{:S(2)}) collective-permute-start(bf16[768,256]{1,0:T(8,128)(2,1)S(1)} %get-tuple-element.28), channel_id=1, source_target_pairs={{0,2},{1,3},{2,0},{3,1},{4,6},{5,7},{6,4},{7,5},{8,10},{9,11},{10,... | collective-permute-start | bytes 1179656 | tf_op jit(solution)/shard_map/ppermute | solution.py:322
  14.8 0.2 collective-permute-start.8
  14.9 0.0 collective-permute-done.2.other_ref
  15.0 1.6 %collective-permute-start.3 = (bf16[384,256]{1,0:T(8,128)(2,1)S(1)}, bf16[384,256]{1,0:T(8,128)(2,1)S(1)}, u32[]{:S(2)}, u32[]{:S(2)}) collective-permute-start(bf16[384,256]{1,0:T(8,128)(2,1)S(1)} %get-tuple-element.36), channel_id=1, source_target_pairs={{0,2},{1,3},{2,0},{3,1},{4,6},{5,7},{6,4},{7,5},{8,10},{9,11},{10,... | collective-permute-start | bytes 589832 | tf_op jit(solution)/shard_map/ppermute | solution.py:336
  16.5 8.2 %collective-permute-done.refs_0_ = bf16[768,256]{1,0:T(8,128)(2,1)S(1)} collective-permute-done((bf16[768,256]{1,0:T(8,128)(2,1)S(1)}, bf16[768,256]{1,0:T(8,128)(2,1)S(1)}, u32[]{:S(2)}, u32[]{:S(2)}) %collective-permute-start) | collective-permute-done | bytes 393248 | tf_op jit(solution)/shard_map/ppermute | solution.py:322
  24.7 0.1 shard_map.65
  24.8 0.1 collective-permute-start.1
  24.9 0.0 collective-permute-done.8.other_ref
  25.0 2.1 %collective-permute-start.9 = (bf16[384,256]{1,0:T(8,128)(2,1)S(1)}, bf16[384,256]{1,0:T(8,128)(2,1)S(1)}, u32[]{:S(2)}, u32[]{:S(2)}) collective-permute-start(bf16[384,256]{1,0:T(8,128)(2,1)S(1)} %get-tuple-element.44), channel_id=1, source_target_pairs={{0,2},{1,3},{2,0},{3,1},{4,6},{5,7},{6,4},{7,5},{8,10},{9,11},{10,... | collective-permute-start | bytes 589832 | tf_op jit(solution)/shard_map/ppermute | solution.py:336
  27.1 1.9 %collective-permute-done.3 = bf16[384,256]{1,0:T(8,128)(2,1)S(1)} collective-permute-done((bf16[384,256]{1,0:T(8,128)(2,1)S(1)}, bf16[384,256]{1,0:T(8,128)(2,1)S(1)}, u32[]{:S(2)}, u32[]{:S(2)}) %collective-permute-start.3) | collective-permute-done | bytes 196640 | tf_op jit(solution)/shard_map/ppermute | solution.py:336
  29.0 0.1 collective-permute-start.4
  29.1 3.8 %collective-permute-done.9 = bf16[384,256]{1,0:T(8,128)(2,1)S(1)} collective-permute-done((bf16[384,256]{1,0:T(8,128)(2,1)S(1)}, bf16[384,256]{1,0:T(8,128)(2,1)S(1)}, u32[]{:S(2)}, u32[]{:S(2)}) %collective-permute-start.9) | collective-permute-done | bytes 196640 | tf_op jit(solution)/shard_map/ppermute | solution.py:336
  33.0 0.1 collective-permute-start.10
  33.0 0.0 collective-permute-done.1.other_ref
  33.1 0.0 copy-done
  33.1 0.0 copy-done.1
  33.1 0.8 %shard_map.66 = (bf16[512,768]{1,0:T(8,128)(2,1)S(1)}, f32[8,128]{1,0:T(8,128)S(1)}) custom-call(s32[1]{0:T(128)} %bitcast.core_ref, s32[1]{0:T(128)} %bitcast.1.tok_ref, s32[4]{0:T(128)S(1)} %copy-done, s32[4]{0:T(128)S(1)} %copy-done.1, f32[768,128]{1,0:T(8,128)S(1)} %get-tuple-element.29.mine_ref, f32[768,128]{1,0:T(8,128)S(1)} %collective-permute-done.1.other_ref), custom_call_target="tpu_custom_call" | custom-call | flops 100000 | tf_op jit(solution)/shard_map/pallas_call | solution.py:154
  33.9 0.0 collective-permute-done.4.other_ref
  33.9 0.4 outer_products.2
  34.3 1.9 %collective-permute-start.5 = (bf16[128,256]{1,0:T(8,128)(2,1)S(1)}, bf16[128,256]{1,0:T(8,128)(2,1)S(1)}, u32[]{:S(2)}, u32[]{:S(2)}) collective-permute-start(bf16[128,256]{1,0:T(8,128)(2,1)S(1)} %get-tuple-element.38), channel_id=1, source_target_pairs={{0,4},{4,0},{8,12},{12,8},{1,5},{5,1},{9,13},{13,9},{2,6},{6,2},{1... | collective-permute-start | bytes 196616 | tf_op jit(solution)/shard_map/ppermute | solution.py:351
  36.2 2.6 %collective-permute-start.6 = (bf16[128,256]{1,0:T(8,128)(2,1)S(1)}, bf16[128,256]{1,0:T(8,128)(2,1)S(1)}, u32[]{:S(2)}, u32[]{:S(2)}) collective-permute-start(bf16[128,256]{1,0:T(8,128)(2,1)S(1)} %get-tuple-element.39), channel_id=1, source_target_pairs={{0,8},{4,12},{8,0},{12,4},{1,9},{5,13},{9,1},{13,5},{2,10},{6,14},... | collective-permute-start | bytes 196616 | tf_op jit(solution)/shard_map/ppermute | solution.py:351
  38.8 0.0 collective-permute-start.7
  38.8 0.0 collective-permute-done.10.other_ref
  38.8 0.4 outer_products.3
  39.2 1.0 %collective-permute-start.11 = (bf16[128,256]{1,0:T(8,128)(2,1)S(1)}, bf16[128,256]{1,0:T(8,128)(2,1)S(1)}, u32[]{:S(2)}, u32[]{:S(2)}) collective-permute-start(bf16[128,256]{1,0:T(8,128)(2,1)S(1)} %get-tuple-element.46), channel_id=1, source_target_pairs={{0,4},{4,0},{8,12},{12,8},{1,5},{5,1},{9,13},{13,9},{2,6},{6,2},{1... | collective-permute-start | bytes 196616 | tf_op jit(solution)/shard_map/ppermute | solution.py:351
  40.2 3.5 %collective-permute-start.12 = (bf16[128,256]{1,0:T(8,128)(2,1)S(1)}, bf16[128,256]{1,0:T(8,128)(2,1)S(1)}, u32[]{:S(2)}, u32[]{:S(2)}) collective-permute-start(bf16[128,256]{1,0:T(8,128)(2,1)S(1)} %get-tuple-element.47), channel_id=1, source_target_pairs={{0,8},{4,12},{8,0},{12,4},{1,9},{5,13},{9,1},{13,5},{2,10},{6,14},... | collective-permute-start | bytes 196616 | tf_op jit(solution)/shard_map/ppermute | solution.py:351
  43.6 0.0 collective-permute-done.5.refs_1_
  43.6 0.0 collective-permute-start.13
  43.6 0.0 collective-permute-done.6.refs_2_
  43.7 1.9 %collective-permute-done.7.refs_3_ = bf16[128,256]{1,0:T(8,128)(2,1)S(1)} collective-permute-done((bf16[128,256]{1,0:T(8,128)(2,1)S(1)}, bf16[128,256]{1,0:T(8,128)(2,1)S(1)}, u32[]{:S(2)}, u32[]{:S(2)}) %collective-permute-start.7) | collective-permute-done | bytes 65568 | tf_op jit(solution)/shard_map/ppermute | solution.py:351
  45.5 0.0 collective-permute-done.11.refs_5_
  45.5 4.6 %collective-permute-done.12.refs_6_ = bf16[128,256]{1,0:T(8,128)(2,1)S(1)} collective-permute-done((bf16[128,256]{1,0:T(8,128)(2,1)S(1)}, bf16[128,256]{1,0:T(8,128)(2,1)S(1)}, u32[]{:S(2)}, u32[]{:S(2)}) %collective-permute-start.12) | collective-permute-done | bytes 65568 | tf_op jit(solution)/shard_map/ppermute | solution.py:351
  50.2 0.0 collective-permute-done.13.refs_7_
  50.2 0.8 %shard_map.70 = f32[1,128,512]{2,1,0:T(8,128)} custom-call(f32[8,128]{1,0:T(8,128)S(1)} %get-tuple-element.31.scale_ref, f32[128,256]{1,0:T(8,128)S(1)} %get-tuple-element.37.refs_0_, bf16[128,256]{1,0:T(8,128)(2,1)S(1)} %collective-permute-done.5.refs_1_, bf16[128,256]{1,0:T(8,128)(2,1)S(1)} %collective-permute-done.6.refs_2_, ...), custom_call_target="tpu_custom_call" | custom-call | flops 100000 | tf_op jit(solution)/shard_map/pallas_call | solution.py:154
  (4 shorter events, 0.2 us)
Async XLA Ops:
  3.4 29.7 %copy-start = (s32[4]{0:T(128)S(1)}, s32[4]{0:T(128)}, u32[]{:S(2)}) copy-start(s32[4]{0:T(128)} %lengths_ref.1) | copy-start | bytes 52
  3.4 29.7 %copy-start.1 = (s32[4]{0:T(128)S(1)}, s32[4]{0:T(128)}, u32[]{:S(2)}) copy-start(s32[4]{0:T(128)} %owner_ref.1) | copy-start | bytes 52
  11.6 3.3 %collective-permute-start.2 = (f32[384,256]{1,0:T(8,128)S(1)}, f32[384,256]{1,0:T(8,128)S(1)}, u32[]{:S(2)}, u32[]{:S(2)}) collective-permute-start(f32[384,256]{1,0:T(8,128)S(1)} %get-tuple-element.34), channel_id=1, source_target_pairs={{0,1},{1,0},{2,3},{3,2},{4,5},{5,4},{6,7},{7,6},{8,9},{9,8},{10,11... | collective-permute-start | bytes 1179656 | tf_op jit(solution)/shard_map/ppermute | solution.py:317
  12.2 12.5 %collective-permute-start = (bf16[768,256]{1,0:T(8,128)(2,1)S(1)}, bf16[768,256]{1,0:T(8,128)(2,1)S(1)}, u32[]{:S(2)}, u32[]{:S(2)}) collective-permute-start(bf16[768,256]{1,0:T(8,128)(2,1)S(1)} %get-tuple-element.28), channel_id=1, source_target_pairs={{0,2},{1,3},{2,0},{3,1},{4,6},{5,7},{6,4},{7,5},{8,10},{9,11},{10,... | collective-permute-start | bytes 1179656 | tf_op jit(solution)/shard_map/ppermute | solution.py:322
  14.8 10.1 %collective-permute-start.8 = (f32[384,256]{1,0:T(8,128)S(1)}, f32[384,256]{1,0:T(8,128)S(1)}, u32[]{:S(2)}, u32[]{:S(2)}) collective-permute-start(f32[384,256]{1,0:T(8,128)S(1)} %get-tuple-element.42), channel_id=1, source_target_pairs={{0,1},{1,0},{2,3},{3,2},{4,5},{5,4},{6,7},{7,6},{8,9},{9,8},{10,11... | collective-permute-start | bytes 1179656 | tf_op jit(solution)/shard_map/ppermute | solution.py:317
  15.0 14.0 %collective-permute-start.3 = (bf16[384,256]{1,0:T(8,128)(2,1)S(1)}, bf16[384,256]{1,0:T(8,128)(2,1)S(1)}, u32[]{:S(2)}, u32[]{:S(2)}) collective-permute-start(bf16[384,256]{1,0:T(8,128)(2,1)S(1)} %get-tuple-element.36), channel_id=1, source_target_pairs={{0,2},{1,3},{2,0},{3,1},{4,6},{5,7},{6,4},{7,5},{8,10},{9,11},{10,... | collective-permute-start | bytes 589832 | tf_op jit(solution)/shard_map/ppermute | solution.py:336
  24.8 8.2 %collective-permute-start.1 = (f32[768,128]{1,0:T(8,128)S(1)}, f32[768,128]{1,0:T(8,128)S(1)}, u32[]{:S(2)}, u32[]{:S(2)}) collective-permute-start(f32[768,128]{1,0:T(8,128)S(1)} %get-tuple-element.30), channel_id=1, source_target_pairs={{0,1},{1,0},{2,3},{3,2},{4,5},{5,4},{6,7},{7,6},{8,9},{9,8},{10,11... | collective-permute-start | bytes 1179656 | tf_op jit(solution)/shard_map/ppermute | solution.py:317
  25.0 7.9 %collective-permute-start.9 = (bf16[384,256]{1,0:T(8,128)(2,1)S(1)}, bf16[384,256]{1,0:T(8,128)(2,1)S(1)}, u32[]{:S(2)}, u32[]{:S(2)}) collective-permute-start(bf16[384,256]{1,0:T(8,128)(2,1)S(1)} %get-tuple-element.44), channel_id=1, source_target_pairs={{0,2},{1,3},{2,0},{3,1},{4,6},{5,7},{6,4},{7,5},{8,10},{9,11},{10,... | collective-permute-start | bytes 589832 | tf_op jit(solution)/shard_map/ppermute | solution.py:336
  29.0 4.9 %collective-permute-start.4 = (bf16[384,256]{1,0:T(8,128)(2,1)S(1)}, bf16[384,256]{1,0:T(8,128)(2,1)S(1)}, u32[]{:S(2)}, u32[]{:S(2)}) collective-permute-start(bf16[384,256]{1,0:T(8,128)(2,1)S(1)} %add_convert_fusion.1.own_ref), channel_id=1, source_target_pairs={{0,1},{1,0},{2,3},{3,2},{4,5},{5,4},{6,7},{7,6},{8,9},{9,8},{10,11... | collective-permute-start | bytes 589832 | tf_op jit(solution)/shard_map/ppermute | solution.py:317
  33.0 5.8 %collective-permute-start.10 = (bf16[384,256]{1,0:T(8,128)(2,1)S(1)}, bf16[384,256]{1,0:T(8,128)(2,1)S(1)}, u32[]{:S(2)}, u32[]{:S(2)}) collective-permute-start(bf16[384,256]{1,0:T(8,128)(2,1)S(1)} %add_convert_fusion.own_ref), channel_id=1, source_target_pairs={{0,1},{1,0},{2,3},{3,2},{4,5},{5,4},{6,7},{7,6},{8,9},{9,8},{10,11... | collective-permute-start | bytes 589832 | tf_op jit(solution)/shard_map/ppermute | solution.py:317
  34.3 9.3 %collective-permute-start.5 = (bf16[128,256]{1,0:T(8,128)(2,1)S(1)}, bf16[128,256]{1,0:T(8,128)(2,1)S(1)}, u32[]{:S(2)}, u32[]{:S(2)}) collective-permute-start(bf16[128,256]{1,0:T(8,128)(2,1)S(1)} %get-tuple-element.38), channel_id=1, source_target_pairs={{0,4},{4,0},{8,12},{12,8},{1,5},{5,1},{9,13},{13,9},{2,6},{6,2},{1... | collective-permute-start | bytes 196616 | tf_op jit(solution)/shard_map/ppermute | solution.py:351
  36.2 7.5 %collective-permute-start.6 = (bf16[128,256]{1,0:T(8,128)(2,1)S(1)}, bf16[128,256]{1,0:T(8,128)(2,1)S(1)}, u32[]{:S(2)}, u32[]{:S(2)}) collective-permute-start(bf16[128,256]{1,0:T(8,128)(2,1)S(1)} %get-tuple-element.39), channel_id=1, source_target_pairs={{0,8},{4,12},{8,0},{12,4},{1,9},{5,13},{9,1},{13,5},{2,10},{6,14},... | collective-permute-start | bytes 196616 | tf_op jit(solution)/shard_map/ppermute | solution.py:351
  38.8 6.8 %collective-permute-start.7 = (bf16[128,256]{1,0:T(8,128)(2,1)S(1)}, bf16[128,256]{1,0:T(8,128)(2,1)S(1)}, u32[]{:S(2)}, u32[]{:S(2)}) collective-permute-start(bf16[128,256]{1,0:T(8,128)(2,1)S(1)} %get-tuple-element.40), channel_id=1, source_target_pairs={{0,12},{4,8},{8,4},{12,0},{1,13},{5,9},{9,5},{13,1},{2,14},{6,10},... | collective-permute-start | bytes 196616 | tf_op jit(solution)/shard_map/ppermute | solution.py:351
  39.2 6.3 %collective-permute-start.11 = (bf16[128,256]{1,0:T(8,128)(2,1)S(1)}, bf16[128,256]{1,0:T(8,128)(2,1)S(1)}, u32[]{:S(2)}, u32[]{:S(2)}) collective-permute-start(bf16[128,256]{1,0:T(8,128)(2,1)S(1)} %get-tuple-element.46), channel_id=1, source_target_pairs={{0,4},{4,0},{8,12},{12,8},{1,5},{5,1},{9,13},{13,9},{2,6},{6,2},{1... | collective-permute-start | bytes 196616 | tf_op jit(solution)/shard_map/ppermute | solution.py:351
  40.2 10.0 %collective-permute-start.12 = (bf16[128,256]{1,0:T(8,128)(2,1)S(1)}, bf16[128,256]{1,0:T(8,128)(2,1)S(1)}, u32[]{:S(2)}, u32[]{:S(2)}) collective-permute-start(bf16[128,256]{1,0:T(8,128)(2,1)S(1)} %get-tuple-element.47), channel_id=1, source_target_pairs={{0,8},{4,12},{8,0},{12,4},{1,9},{5,13},{9,1},{13,5},{2,10},{6,14},... | collective-permute-start | bytes 196616 | tf_op jit(solution)/shard_map/ppermute | solution.py:351
  43.6 6.5 %collective-permute-start.13 = (bf16[128,256]{1,0:T(8,128)(2,1)S(1)}, bf16[128,256]{1,0:T(8,128)(2,1)S(1)}, u32[]{:S(2)}, u32[]{:S(2)}) collective-permute-start(bf16[128,256]{1,0:T(8,128)(2,1)S(1)} %get-tuple-element.48), channel_id=1, source_target_pairs={{0,12},{4,8},{8,4},{12,0},{1,13},{5,9},{9,5},{13,1},{2,14},{6,10},... | collective-permute-start | bytes 196616 | tf_op jit(solution)/shard_map/ppermute | solution.py:351

commit v4 on v3

--- a/solution.py
+++ b/solution.py
@@ -10,6 +10,8 @@
 
 CHUNKS = 2
 TILE = 512
+NEAR_TILE = 1024
+NEAR_AHEAD = 4
 AHEAD = 8
 MIB = 1 << 20
 
@@ -40,37 +42,42 @@
     return tile
 
 
-def stream(far, near, far_w, near_w, sems):
-    depth = near_w.shape[0]
-    tile = depth_tile(depth, TILE)
-    count = depth // tile
-
-    def lines(t):
-        return pl.ds(t * tile, tile)
+def tiles(depth, most):
+    tile = depth_tile(depth, most)
+    lengths = [tile] * (depth // tile)
+    if tile % 512 == 0 and tile > 512:
+        lengths[:1] = [tile // 4, tile // 4, tile // 2]
+    return [(sum(lengths[:t]), length) for t, length in enumerate(lengths)]
+
+
+def stream(far, near, far_w, near_w, sems, most, ahead):
+    lines = [pl.ds(begin, length) for begin, length in tiles(near_w.shape[0], most)]
 
     def copies(t):
-        return (
-            pltpu.make_async_copy(far_w.at[lines(t), :], near_w.at[lines(t), :], sems.at[0, t]),
-            pltpu.make_async_copy(far.at[:, lines(t)], near.at[:, lines(t)], sems.at[1, t]),
-        )
+        pair = [pltpu.make_async_copy(far.at[:, lines[t]], near.at[:, lines[t]], sems.at[1, t])]
+        if far_w is not None:
+            pair.append(
+                pltpu.make_async_copy(far_w.at[lines[t], :], near_w.at[lines[t], :], sems.at[0, t])
+            )
+        return pair
 
     def start(t):
         for copy in copies(t):
             copy.start()
 
-    for t in range(min(AHEAD, count)):
+    for t in range(min(ahead, len(lines))):
         start(t)
-    for t in range(count):
+    for t in range(len(lines)):
         for copy in copies(t):
             copy.wait()
-        if t + AHEAD < count:
-            start(t + AHEAD)
-        yield lines(t), t == 0, t + 1 == count
-
-
-def grads_kernel(chips, chip_ref, a_hbm, w_hbm, near_ref, *refs):
+        if t + ahead < len(lines):
+            start(t + ahead)
+        yield lines[t], t == 0, t + 1 == len(lines)
+
+
+def grads_kernel(chips, a_hbm, w_hbm, near_ref, *refs):
     far_refs, (a_ref, w_ref, total, sems) = refs[:-4], refs[-4:]
-    for lines, begins, _ in stream(a_hbm, a_ref, w_hbm, w_ref, sems):
+    for lines, begins, _ in stream(a_hbm, a_ref, w_hbm, w_ref, sems, TILE, AHEAD):
         product = jnp.dot(a_ref[:, lines], w_ref[lines, :], preferred_element_type=jnp.float32)
         if begins:
             total[...] = product
@@ -79,7 +86,7 @@
     width = near_ref.shape[1]
     for chip in range(chips):
 
-        @pl.when(chip_ref[0] == chip)
+        @pl.when(lax.axis_index("feat") // 2 == chip)
         def _():
             near_ref[...] = total[:, pl.ds(chip * width, width)]
             for step, ref in enumerate(far_refs):
@@ -87,10 +94,11 @@
                 ref[...] = total[:, pl.ds(place, width)].astype(ref.dtype)
 
 
-def acts_kernel(core_ref, a_hbm, w_hbm, after_ref, *refs):
-    halves, (a_ref, w_ref, total, sems) = refs[:-4], refs[-4:]
+def acts_kernel(a_hbm, w_ref, after_ref, *refs):
+    core = lax.rem(lax.axis_index("feat"), 2)
+    halves, (a_ref, _, total, sems) = refs[:-4], refs[-4:]
     half, width = halves[0].shape
-    for lines, begins, ends in stream(a_hbm, a_ref, w_hbm, w_ref, sems):
+    for lines, begins, ends in stream(a_hbm, a_ref, None, w_ref, sems, NEAR_TILE, NEAR_AHEAD):
         if not ends:
             product = jnp.dot(a_ref[:, lines], w_ref[lines, :], preferred_element_type=jnp.float32)
             if begins:
@@ -98,55 +106,58 @@
             else:
                 total[...] += product
             continue
-        for side in range(2):
-            place = core_ref[0] if side == 0 else 1 - core_ref[0]
-            rows = pl.ds(pl.multiple_of(place * half, half), half)
-            result = jnp.dot(a_ref[rows, lines], w_ref[lines, :], preferred_element_type=jnp.float32)
-            if not begins:
-                result = total[rows, :] + result
-            for chunk in range(len(halves) // 2):
-                halves[2 * chunk + side][...] = result[:, chunk * width : (chunk + 1) * width]
-
-
-def product_call(kernel, scalar, a, w, after, out):
+        for chunk in range(len(halves) // 2):
+            columns = pl.ds(chunk * width, width)
+            for side in range(2):
+                place = core if side == 0 else 1 - core
+                rows = pl.ds(pl.multiple_of(place * half, half), half)
+                result = jnp.dot(
+                    a_ref[rows, lines], w_ref[lines, columns], preferred_element_type=jnp.float32
+                )
+                if not begins:
+                    result = total[rows, columns] + result
+                halves[2 * chunk + side][...] = result
+
+
+def product_call(kernel, a, w, after, out):
     rows, depth = a.shape
     rank = w.shape[1]
     return pl.pallas_call(
         kernel,
-        in_specs=[pl.BlockSpec(memory_space=pltpu.SMEM)]
-        + [pl.BlockSpec(memory_space=pltpu.HBM)] * 2
+        in_specs=[pl.BlockSpec(memory_space=pltpu.HBM)]
+        + [pl.BlockSpec(memory_space=pltpu.VMEM if after else pltpu.HBM)]
         + [pl.BlockSpec(memory_space=pl.ANY)] * len(after),
         out_specs=[pl.BlockSpec(memory_space=pltpu.VMEM)] * len(out),
         out_shape=out,
         scratch_shapes=[
             pltpu.VMEM((rows, depth), a.dtype),
-            pltpu.VMEM((depth, rank), w.dtype),
+            pltpu.VMEM((8, rank) if after else (depth, rank), w.dtype),
             pltpu.VMEM((rows, rank), jnp.float32),
-            pltpu.SemaphoreType.DMA((2, depth // depth_tile(depth, TILE))),
+            pltpu.SemaphoreType.DMA((2, len(tiles(depth, NEAR_TILE if after else TILE)))),
         ],
         compiler_params=pltpu.CompilerParams(
-            vmem_limit_bytes=2 * depth * (rows + rank) + 4 * rows * rank + 3 * MIB
+            vmem_limit_bytes=2 * depth * (rows + (0 if after else rank)) + 4 * rows * rank + 3 * MIB
         ),
         cost_estimate=pl.CostEstimate(
-            flops=2 * rows * depth * rank,
-            bytes_accessed=2 * (rows + rank) * depth,
+            flops=2 * rows * depth * rank * (1 if after else 10),
+            bytes_accessed=0,
             transcendentals=0,
         ),
-    )(scalar, a, w, *after)
-
-
-def project_grads(grads, proj_out, chip, chips):
+    )(a, w, *after)
+
+
+def project_grads(grads, proj_out, chips):
     rows, rank = grads.shape[0], proj_out.shape[1]
     width = rank // chips
     out = [pltpu.VMEM((rows, width), jnp.float32)]
     out += [pltpu.VMEM((rows, width), jnp.bfloat16)] * (chips - 1)
-    return product_call(functools.partial(grads_kernel, chips), chip, grads, proj_out, [], out)
-
-
-def project_acts(acts, proj_in, core, after):
+    return product_call(functools.partial(grads_kernel, chips), grads, proj_out, [], out)
+
+
+def project_acts(acts, proj_in, after):
     rows, rank = acts.shape[0], proj_in.shape[1]
     out = [pltpu.VMEM((rows // 2, rank // CHUNKS), jnp.float32)] * (2 * CHUNKS)
-    return product_call(acts_kernel, core, acts, proj_in, [after], out)
+    return product_call(acts_kernel, acts, proj_in, [after], out)
 
 
 def vmem_call(kernel, scalars, arrays, out, limit=6, flops=10**5):
@@ -162,12 +173,12 @@
     )(*scalars, *arrays)
 
 
-def chip_sum_kernel(core_ref, near_ref, *refs):
+def chip_sum_kernel(near_ref, *refs):
     far_refs, (mine_ref, theirs_ref) = refs[:-2], refs[-2:]
     share = mine_ref.shape[1]
     for which in range(2):
 
-        @pl.when(core_ref[0] == which)
+        @pl.when(lax.rem(lax.axis_index("feat"), 2) == which)
         def _():
             for side, out_ref in ((which, mine_ref), (1 - which, theirs_ref)):
                 place = pl.ds(side * share, share)
@@ -184,13 +195,13 @@
 
 
 def spread_kernel(
-    tok_count, core_ref, tok_ref, lengths_ref, owner_ref, mine_ref, other_ref, out_ref, scale_ref
+    tok_count, lengths_ref, owner_ref, mine_ref, other_ref, out_ref, scale_ref
 ):
     rows, share = mine_ref.shape
     docs = lengths_ref.shape[0]
     slots = docs // tok_count
     half = rows // 2
-    tok, core = tok_ref[0], core_ref[0]
+    tok, core = lax.axis_index("tok"), lax.rem(lax.axis_index("feat"), 2)
     starts, ends, targets = [], [], []
     seen = jnp.int32(0)
     for d in range(docs):
@@ -229,12 +240,12 @@
                 )
 
 
-def spread(mine, other, core, tok, doc_lengths, doc_owner, tok_count):
+def spread(mine, other, doc_lengths, doc_owner, tok_count):
     rows, share = mine.shape
     docs = doc_lengths.shape[0]
     return vmem_call(
         functools.partial(spread_kernel, tok_count),
-        (core, tok, doc_lengths, doc_owner),
+        (doc_lengths, doc_owner),
         (mine, other),
         [
             pltpu.VMEM((docs * share, rows), jnp.bfloat16),
@@ -303,24 +314,20 @@
     tok_count = lax.axis_size("tok")
     feat_count = lax.axis_size("feat")
     chips = feat_count // 2
-    feat = lax.axis_index("feat")
-    chip = feat // 2
-    core = (feat % 2).reshape(1)
-    tok = lax.axis_index("tok").reshape(1)
     share = rank // feat_count
     rows = acts.shape[0]
-    acts, grads, proj_in, proj_out = (
-        pltpu.with_memory_space_constraint(v, pltpu.HBM) for v in (acts, grads, proj_in, proj_out)
+    acts, grads, proj_out = (
+        pltpu.with_memory_space_constraint(v, pltpu.HBM) for v in (acts, grads, proj_out)
     )
 
     def swap(value):
         return lax.ppermute(value, "feat", partner_pairs(feat_count))
 
-    near, *far = project_grads(grads, proj_out, chip.reshape(1), chips)
+    near, *far = project_grads(grads, proj_out, chips)
     arrived = []
     for step in range(1, chips):
         arrived.append(lax.ppermute(far[step - 1], "feat", chip_shift(feat_count, step)))
-    halves = project_acts(acts, proj_in, core, near)
+    halves = project_acts(acts, proj_in, near)
 
     lows = []
     for chunk in range(CHUNKS):
@@ -338,10 +345,10 @@
         lows.append(full_in.astype(jnp.bfloat16))
 
     mine, theirs = vmem_call(
-        chip_sum_kernel, (core,), (near, *arrived), [pltpu.VMEM((rows, share), jnp.float32)] * 2
+        chip_sum_kernel, (), (near, *arrived), [pltpu.VMEM((rows, share), jnp.float32)] * 2
     )
     other = swap(theirs)
-    spread_low, scale = spread(mine, other, core, tok, doc_lengths, doc_owner, tok_count)
+    spread_low, scale = spread(mine, other, doc_lengths, doc_owner, tok_count)
     parts = []
     for low_in in lows:
         other = swap(low_in)

time: 51.1 us -> 51.7 us (1.012)
  local copies, waits for them, and re-layouts: 0.01 us -> 1.15 us
    unnamed x4 -> x6, local copies, waits for them, and re-layouts: 0.01 us -> 1.15 us
where the time goes in v4:
time: 51.7 us; the launch traced here: 51.6 us
  waiting for transfers between devices  20.4 us (39%)
  starting transfers between devices  16.1 us (31%)
  Pallas kernels  13.7 us (26%)
  local copies, waits for them, and re-layouts  1.15 us (2%)
    pallas_call x2, Pallas kernels, product_call(): pl.pallas_call(kernel, in_specs=[pl.BlockSpec(memory_space=pltpu.HBM)] +...  11.1 us
    ppermute x6, starting transfers between devices, shards(): lax.ppermute(sends[step - 1], 'tok', exchange(tok_count, step))  8.96 us
    ppermute x1, waiting for transfers between devices, shards(): lax.ppermute(far[step - 1], 'feat', chip_shift(feat_count, step))  8.21 us
    ppermute x6, waiting for transfers between devices, shards(): lax.ppermute(sends[step - 1], 'tok', exchange(tok_count, step))  6.53 us
    ppermute x2, waiting for transfers between devices, shards(): other = lax.ppermute(sent, 'feat', chip_shift(feat_count, step))  5.7 us
    ppermute x2, starting transfers between devices, shards(): other = lax.ppermute(sent, 'feat', chip_shift(feat_count, step))  3.64 us
    ppermute x1, starting transfers between devices, shards(): lax.ppermute(far[step - 1], 'feat', chip_shift(feat_count, step))  2.53 us
    pallas_call x5, Pallas kernels, vmem_call(): pl.pallas_call(kernel, in_specs=[pl.BlockSpec(memory_space=pltpu.SMEM)] *...  1.76 us
  transfers between devices with their start and end apart: 14, of which 5 were waited for; matrix products, arithmetic and copies ran while one was open for 0% of the time, Pallas kernels for 4%

profile of v4, /device:TPU:0, one launch (start us, length us, event | category | flops | bytes accessed | tf_op | source)
XLA Modules:
  0.0 51.6 jit_solution(5530791501465736155)
XLA Ops:
  0.0 0.0 copy-start.2
  0.0 3.5 %shard_map.64 = (f32[768,256]{1,0:T(8,128)S(1)}, bf16[768,256]{1,0:T(8,128)(2,1)S(1)}) custom-call(bf16[768,2048]{1,0:T(8,128)(2,1)} %a_hbm.2, bf16[2048,512]{1,0:T(8,128)(2,1)} %w_hbm.1), custom_call_target="tpu_custom_call" | custom-call | flops 16106127360 | tf_op jit(solution)/shard_map/pallas_call | solution.py:125
  3.5 1.1 %copy-done.2 = bf16[7168,512]{1,0:T(8,128)(2,1)S(1)} copy-done((bf16[7168,512]{1,0:T(8,128)(2,1)S(1)}, bf16[7168,512]{1,0:T(8,128)(2,1)}, u32[]{:S(2)}) %copy-start.2) | copy-done | bytes 7340056
  4.7 0.0 copy-start
  4.7 0.0 copy-start.1
  4.7 7.6 %shard_map.67 = (f32[384,256]{1,0:T(8,128)S(1)}, f32[384,256]{1,0:T(8,128)S(1)}, f32[384,256]{1,0:T(8,128)S(1)}, f32[384,256]{1,0:T(8,128)S(1)}) custom-call(bf16[768,7168]{1,0:T(8,128)(2,1)} %a_hbm.3, bf16[7168,512]{1,0:T(8,128)(2,1)S(1)} %copy-done.2, f32[768,256]{1,0:T(8,128)S(1)} %get-tuple-element.27.near_ref.after_ref), custom_call_target="tpu_custom_call" | custom-call | flops 5637144576 | tf_op jit(solution)/shard_map/pallas_call | solution.py:125
  12.3 0.6 %collective-permute-start.2 = (f32[384,256]{1,0:T(8,128)S(1)}, f32[384,256]{1,0:T(8,128)S(1)}, u32[]{:S(2)}, u32[]{:S(2)}) collective-permute-start(f32[384,256]{1,0:T(8,128)S(1)} %get-tuple-element.34), channel_id=1, source_target_pairs={{0,1},{1,0},{2,3},{3,2},{4,5},{5,4},{6,7},{7,6},{8,9},{9,8},{10,11... | collective-permute-start | bytes 1179656 | tf_op jit(solution)/shard_map/ppermute | solution.py:324
  12.8 2.5 %collective-permute-start = (bf16[768,256]{1,0:T(8,128)(2,1)S(1)}, bf16[768,256]{1,0:T(8,128)(2,1)S(1)}, u32[]{:S(2)}, u32[]{:S(2)}) collective-permute-start(bf16[768,256]{1,0:T(8,128)(2,1)S(1)} %get-tuple-element.28), channel_id=1, source_target_pairs={{0,2},{1,3},{2,0},{3,1},{4,6},{5,7},{6,4},{7,5},{8,10},{9,11},{10,... | collective-permute-start | bytes 1179656 | tf_op jit(solution)/shard_map/ppermute | solution.py:329
  15.3 0.2 collective-permute-start.8
  15.5 0.0 collective-permute-done.2.other_ref
  15.6 1.6 %collective-permute-start.3 = (bf16[384,256]{1,0:T(8,128)(2,1)S(1)}, bf16[384,256]{1,0:T(8,128)(2,1)S(1)}, u32[]{:S(2)}, u32[]{:S(2)}) collective-permute-start(bf16[384,256]{1,0:T(8,128)(2,1)S(1)} %get-tuple-element.36), channel_id=1, source_target_pairs={{0,2},{1,3},{2,0},{3,1},{4,6},{5,7},{6,4},{7,5},{8,10},{9,11},{10,... | collective-permute-start | bytes 589832 | tf_op jit(solution)/shard_map/ppermute | solution.py:343
  17.1 8.2 %collective-permute-done.refs_0_ = bf16[768,256]{1,0:T(8,128)(2,1)S(1)} collective-permute-done((bf16[768,256]{1,0:T(8,128)(2,1)S(1)}, bf16[768,256]{1,0:T(8,128)(2,1)S(1)}, u32[]{:S(2)}, u32[]{:S(2)}) %collective-permute-start) | collective-permute-done | bytes 393248 | tf_op jit(solution)/shard_map/ppermute | solution.py:329
  25.3 0.1 shard_map.65
  25.4 0.1 collective-permute-start.1
  25.5 0.0 collective-permute-done.8.other_ref
  25.5 0.1 shard_map.69
  25.6 2.1 %collective-permute-start.9 = (bf16[384,256]{1,0:T(8,128)(2,1)S(1)}, bf16[384,256]{1,0:T(8,128)(2,1)S(1)}, u32[]{:S(2)}, u32[]{:S(2)}) collective-permute-start(bf16[384,256]{1,0:T(8,128)(2,1)S(1)} %get-tuple-element.44), channel_id=1, source_target_pairs={{0,2},{1,3},{2,0},{3,1},{4,6},{5,7},{6,4},{7,5},{8,10},{9,11},{10,... | collective-permute-start | bytes 589832 | tf_op jit(solution)/shard_map/ppermute | solution.py:343
  27.7 1.9 %collective-permute-done.3 = bf16[384,256]{1,0:T(8,128)(2,1)S(1)} collective-permute-done((bf16[384,256]{1,0:T(8,128)(2,1)S(1)}, bf16[384,256]{1,0:T(8,128)(2,1)S(1)}, u32[]{:S(2)}, u32[]{:S(2)}) %collective-permute-start.3) | collective-permute-done | bytes 196640 | tf_op jit(solution)/shard_map/ppermute | solution.py:343
  29.6 0.1 collective-permute-start.4
  29.7 3.8 %collective-permute-done.9 = bf16[384,256]{1,0:T(8,128)(2,1)S(1)} collective-permute-done((bf16[384,256]{1,0:T(8,128)(2,1)S(1)}, bf16[384,256]{1,0:T(8,128)(2,1)S(1)}, u32[]{:S(2)}, u32[]{:S(2)}) %collective-permute-start.9) | collective-permute-done | bytes 196640 | tf_op jit(solution)/shard_map/ppermute | solution.py:343
  33.5 0.1 collective-permute-start.10
  33.6 0.0 collective-permute-done.1.other_ref
  33.6 0.0 copy-done
  33.6 0.0 copy-done.1
  33.6 0.8 %shard_map.66 = (bf16[512,768]{1,0:T(8,128)(2,1)S(1)}, f32[8,128]{1,0:T(8,128)S(1)}) custom-call(s32[4]{0:T(128)S(1)} %copy-done, s32[4]{0:T(128)S(1)} %copy-done.1, f32[768,128]{1,0:T(8,128)S(1)} %get-tuple-element.29.mine_ref, f32[768,128]{1,0:T(8,128)S(1)} %collective-permute-done.1.other_ref), custom_call_target="tpu_custom_call" | custom-call | flops 100000 | tf_op jit(solution)/shard_map/pallas_call | solution.py:165
  34.4 0.0 collective-permute-done.4.other_ref
  34.4 0.4 outer_products.2
  34.9 1.9 %collective-permute-start.5 = (bf16[128,256]{1,0:T(8,128)(2,1)S(1)}, bf16[128,256]{1,0:T(8,128)(2,1)S(1)}, u32[]{:S(2)}, u32[]{:S(2)}) collective-permute-start(bf16[128,256]{1,0:T(8,128)(2,1)S(1)} %get-tuple-element.38), channel_id=1, source_target_pairs={{0,4},{4,0},{8,12},{12,8},{1,5},{5,1},{9,13},{13,9},{2,6},{6,2},{1... | collective-permute-start | bytes 196616 | tf_op jit(solution)/shard_map/ppermute | solution.py:358
  36.8 2.6 %collective-permute-start.6 = (bf16[128,256]{1,0:T(8,128)(2,1)S(1)}, bf16[128,256]{1,0:T(8,128)(2,1)S(1)}, u32[]{:S(2)}, u32[]{:S(2)}) collective-permute-start(bf16[128,256]{1,0:T(8,128)(2,1)S(1)} %get-tuple-element.39), channel_id=1, source_target_pairs={{0,8},{4,12},{8,0},{12,4},{1,9},{5,13},{9,1},{13,5},{2,10},{6,14},... | collective-permute-start | bytes 196616 | tf_op jit(solution)/shard_map/ppermute | solution.py:358
  39.4 0.0 collective-permute-start.7
  39.4 0.0 collective-permute-done.10.other_ref
  39.4 0.4 outer_products.3
  39.8 1.0 %collective-permute-start.11 = (bf16[128,256]{1,0:T(8,128)(2,1)S(1)}, bf16[128,256]{1,0:T(8,128)(2,1)S(1)}, u32[]{:S(2)}, u32[]{:S(2)}) collective-permute-start(bf16[128,256]{1,0:T(8,128)(2,1)S(1)} %get-tuple-element.46), channel_id=1, source_target_pairs={{0,4},{4,0},{8,12},{12,8},{1,5},{5,1},{9,13},{13,9},{2,6},{6,2},{1... | collective-permute-start | bytes 196616 | tf_op jit(solution)/shard_map/ppermute | solution.py:358
  40.8 3.5 %collective-permute-start.12 = (bf16[128,256]{1,0:T(8,128)(2,1)S(1)}, bf16[128,256]{1,0:T(8,128)(2,1)S(1)}, u32[]{:S(2)}, u32[]{:S(2)}) collective-permute-start(bf16[128,256]{1,0:T(8,128)(2,1)S(1)} %get-tuple-element.47), channel_id=1, source_target_pairs={{0,8},{4,12},{8,0},{12,4},{1,9},{5,13},{9,1},{13,5},{2,10},{6,14},... | collective-permute-start | bytes 196616 | tf_op jit(solution)/shard_map/ppermute | solution.py:358
  44.3 0.0 collective-permute-done.5.refs_1_
  44.3 0.0 collective-permute-start.13
  44.3 0.0 collective-permute-done.6.refs_2_
  44.3 1.9 %collective-permute-done.7.refs_3_ = bf16[128,256]{1,0:T(8,128)(2,1)S(1)} collective-permute-done((bf16[128,256]{1,0:T(8,128)(2,1)S(1)}, bf16[128,256]{1,0:T(8,128)(2,1)S(1)}, u32[]{:S(2)}, u32[]{:S(2)}) %collective-permute-start.7) | collective-permute-done | bytes 65568 | tf_op jit(solution)/shard_map/ppermute | solution.py:358
  46.1 0.0 collective-permute-done.11.refs_5_
  46.1 4.7 %collective-permute-done.12.refs_6_ = bf16[128,256]{1,0:T(8,128)(2,1)S(1)} collective-permute-done((bf16[128,256]{1,0:T(8,128)(2,1)S(1)}, bf16[128,256]{1,0:T(8,128)(2,1)S(1)}, u32[]{:S(2)}, u32[]{:S(2)}) %collective-permute-start.12) | collective-permute-done | bytes 65568 | tf_op jit(solution)/shard_map/ppermute | solution.py:358
  50.8 0.0 collective-permute-done.13.refs_7_
  50.8 0.8 %shard_map.70 = f32[1,128,512]{2,1,0:T(8,128)} custom-call(f32[8,128]{1,0:T(8,128)S(1)} %get-tuple-element.31.scale_ref, f32[128,256]{1,0:T(8,128)S(1)} %get-tuple-element.37.refs_0_, bf16[128,256]{1,0:T(8,128)(2,1)S(1)} %collective-permute-done.5.refs_1_, bf16[128,256]{1,0:T(8,128)(2,1)S(1)} %collective-permute-done.6.refs_2_, ...), custom_call_target="tpu_custom_call" | custom-call | flops 100000 | tf_op jit(solution)/shard_map/pallas_call | solution.py:165
  (3 shorter events, 0.1 us)
Async XLA Ops:
  0.0 4.7 %copy-start.2 = (bf16[7168,512]{1,0:T(8,128)(2,1)S(1)}, bf16[7168,512]{1,0:T(8,128)(2,1)}, u32[]{:S(2)}) copy-start(bf16[7168,512]{1,0:T(8,128)(2,1)} %w_ref.1) | copy-start | bytes 22020100
  4.7 28.9 %copy-start = (s32[4]{0:T(128)S(1)}, s32[4]{0:T(128)}, u32[]{:S(2)}) copy-start(s32[4]{0:T(128)} %lengths_ref.1) | copy-start | bytes 52
  4.7 28.9 %copy-start.1 = (s32[4]{0:T(128)S(1)}, s32[4]{0:T(128)}, u32[]{:S(2)}) copy-start(s32[4]{0:T(128)} %owner_ref.1) | copy-start | bytes 52
  12.3 3.2 %collective-permute-start.2 = (f32[384,256]{1,0:T(8,128)S(1)}, f32[384,256]{1,0:T(8,128)S(1)}, u32[]{:S(2)}, u32[]{:S(2)}) collective-permute-start(f32[384,256]{1,0:T(8,128)S(1)} %get-tuple-element.34), channel_id=1, source_target_pairs={{0,1},{1,0},{2,3},{3,2},{4,5},{5,4},{6,7},{7,6},{8,9},{9,8},{10,11... | collective-permute-start | bytes 1179656 | tf_op jit(solution)/shard_map/ppermute | solution.py:324
  12.8 12.5 %collective-permute-start = (bf16[768,256]{1,0:T(8,128)(2,1)S(1)}, bf16[768,256]{1,0:T(8,128)(2,1)S(1)}, u32[]{:S(2)}, u32[]{:S(2)}) collective-permute-start(bf16[768,256]{1,0:T(8,128)(2,1)S(1)} %get-tuple-element.28), channel_id=1, source_target_pairs={{0,2},{1,3},{2,0},{3,1},{4,6},{5,7},{6,4},{7,5},{8,10},{9,11},{10,... | collective-permute-start | bytes 1179656 | tf_op jit(solution)/shard_map/ppermute | solution.py:329
  15.3 10.1 %collective-permute-start.8 = (f32[384,256]{1,0:T(8,128)S(1)}, f32[384,256]{1,0:T(8,128)S(1)}, u32[]{:S(2)}, u32[]{:S(2)}) collective-permute-start(f32[384,256]{1,0:T(8,128)S(1)} %get-tuple-element.42), channel_id=1, source_target_pairs={{0,1},{1,0},{2,3},{3,2},{4,5},{5,4},{6,7},{7,6},{8,9},{9,8},{10,11... | collective-permute-start | bytes 1179656 | tf_op jit(solution)/shard_map/ppermute | solution.py:324
  15.6 14.0 %collective-permute-start.3 = (bf16[384,256]{1,0:T(8,128)(2,1)S(1)}, bf16[384,256]{1,0:T(8,128)(2,1)S(1)}, u32[]{:S(2)}, u32[]{:S(2)}) collective-permute-start(bf16[384,256]{1,0:T(8,128)(2,1)S(1)} %get-tuple-element.36), channel_id=1, source_target_pairs={{0,2},{1,3},{2,0},{3,1},{4,6},{5,7},{6,4},{7,5},{8,10},{9,11},{10,... | collective-permute-start | bytes 589832 | tf_op jit(solution)/shard_map/ppermute | solution.py:343
  25.4 8.2 %collective-permute-start.1 = (f32[768,128]{1,0:T(8,128)S(1)}, f32[768,128]{1,0:T(8,128)S(1)}, u32[]{:S(2)}, u32[]{:S(2)}) collective-permute-start(f32[768,128]{1,0:T(8,128)S(1)} %get-tuple-element.30), channel_id=1, source_target_pairs={{0,1},{1,0},{2,3},{3,2},{4,5},{5,4},{6,7},{7,6},{8,9},{9,8},{10,11... | collective-permute-start | bytes 1179656 | tf_op jit(solution)/shard_map/ppermute | solution.py:324
  25.6 7.9 %collective-permute-start.9 = (bf16[384,256]{1,0:T(8,128)(2,1)S(1)}, bf16[384,256]{1,0:T(8,128)(2,1)S(1)}, u32[]{:S(2)}, u32[]{:S(2)}) collective-permute-start(bf16[384,256]{1,0:T(8,128)(2,1)S(1)} %get-tuple-element.44), channel_id=1, source_target_pairs={{0,2},{1,3},{2,0},{3,1},{4,6},{5,7},{6,4},{7,5},{8,10},{9,11},{10,... | collective-permute-start | bytes 589832 | tf_op jit(solution)/shard_map/ppermute | solution.py:343
  29.6 4.9 %collective-permute-start.4 = (bf16[384,256]{1,0:T(8,128)(2,1)S(1)}, bf16[384,256]{1,0:T(8,128)(2,1)S(1)}, u32[]{:S(2)}, u32[]{:S(2)}) collective-permute-start(bf16[384,256]{1,0:T(8,128)(2,1)S(1)} %add_convert_fusion.1.own_ref), channel_id=1, source_target_pairs={{0,1},{1,0},{2,3},{3,2},{4,5},{5,4},{6,7},{7,6},{8,9},{9,8},{10,11... | collective-permute-start | bytes 589832 | tf_op jit(solution)/shard_map/ppermute | solution.py:324
  33.5 5.9 %collective-permute-start.10 = (bf16[384,256]{1,0:T(8,128)(2,1)S(1)}, bf16[384,256]{1,0:T(8,128)(2,1)S(1)}, u32[]{:S(2)}, u32[]{:S(2)}) collective-permute-start(bf16[384,256]{1,0:T(8,128)(2,1)S(1)} %add_convert_fusion.own_ref), channel_id=1, source_target_pairs={{0,1},{1,0},{2,3},{3,2},{4,5},{5,4},{6,7},{7,6},{8,9},{9,8},{10,11... | collective-permute-start | bytes 589832 | tf_op jit(solution)/shard_map/ppermute | solution.py:324
  34.9 9.4 %collective-permute-start.5 = (bf16[128,256]{1,0:T(8,128)(2,1)S(1)}, bf16[128,256]{1,0:T(8,128)(2,1)S(1)}, u32[]{:S(2)}, u32[]{:S(2)}) collective-permute-start(bf16[128,256]{1,0:T(8,128)(2,1)S(1)} %get-tuple-element.38), channel_id=1, source_target_pairs={{0,4},{4,0},{8,12},{12,8},{1,5},{5,1},{9,13},{13,9},{2,6},{6,2},{1... | collective-permute-start | bytes 196616 | tf_op jit(solution)/shard_map/ppermute | solution.py:358
  36.8 7.5 %collective-permute-start.6 = (bf16[128,256]{1,0:T(8,128)(2,1)S(1)}, bf16[128,256]{1,0:T(8,128)(2,1)S(1)}, u32[]{:S(2)}, u32[]{:S(2)}) collective-permute-start(bf16[128,256]{1,0:T(8,128)(2,1)S(1)} %get-tuple-element.39), channel_id=1, source_target_pairs={{0,8},{4,12},{8,0},{12,4},{1,9},{5,13},{9,1},{13,5},{2,10},{6,14},... | collective-permute-start | bytes 196616 | tf_op jit(solution)/shard_map/ppermute | solution.py:358
  39.4 6.8 %collective-permute-start.7 = (bf16[128,256]{1,0:T(8,128)(2,1)S(1)}, bf16[128,256]{1,0:T(8,128)(2,1)S(1)}, u32[]{:S(2)}, u32[]{:S(2)}) collective-permute-start(bf16[128,256]{1,0:T(8,128)(2,1)S(1)} %get-tuple-element.40), channel_id=1, source_target_pairs={{0,12},{4,8},{8,4},{12,0},{1,13},{5,9},{9,5},{13,1},{2,14},{6,10},... | collective-permute-start | bytes 196616 | tf_op jit(solution)/shard_map/ppermute | solution.py:358
  39.8 6.3 %collective-permute-start.11 = (bf16[128,256]{1,0:T(8,128)(2,1)S(1)}, bf16[128,256]{1,0:T(8,128)(2,1)S(1)}, u32[]{:S(2)}, u32[]{:S(2)}) collective-permute-start(bf16[128,256]{1,0:T(8,128)(2,1)S(1)} %get-tuple-element.46), channel_id=1, source_target_pairs={{0,4},{4,0},{8,12},{12,8},{1,5},{5,1},{9,13},{13,9},{2,6},{6,2},{1... | collective-permute-start | bytes 196616 | tf_op jit(solution)/shard_map/ppermute | solution.py:358
  40.8 10.0 %collective-permute-start.12 = (bf16[128,256]{1,0:T(8,128)(2,1)S(1)}, bf16[128,256]{1,0:T(8,128)(2,1)S(1)}, u32[]{:S(2)}, u32[]{:S(2)}) collective-permute-start(bf16[128,256]{1,0:T(8,128)(2,1)S(1)} %get-tuple-element.47), channel_id=1, source_target_pairs={{0,8},{4,12},{8,0},{12,4},{1,9},{5,13},{9,1},{13,5},{2,10},{6,14},... | collective-permute-start | bytes 196616 | tf_op jit(solution)/shard_map/ppermute | solution.py:358
  44.3 6.5 %collective-permute-start.13 = (bf16[128,256]{1,0:T(8,128)(2,1)S(1)}, bf16[128,256]{1,0:T(8,128)(2,1)S(1)}, u32[]{:S(2)}, u32[]{:S(2)}) collective-permute-start(bf16[128,256]{1,0:T(8,128)(2,1)S(1)} %get-tuple-element.48), channel_id=1, source_target_pairs={{0,12},{4,8},{8,4},{12,0},{1,13},{5,9},{9,5},{13,1},{2,14},{6,10},... | collective-permute-start | bytes 196616 | tf_op jit(solution)/shard_map/ppermute | solution.py:358
